TPU v7x, 256 devices: a whole 4x4x8 slice. The times are simulated.
256 devices in a mesh: blk: 16 (over z, core), section: 16 (over y, x).
Axes of the slice: x: 4, y: 4, z: 8, core: 2. Of those that a mesh axis runs over, the one named last changes fastest.
Arguments:
- hidden: bfloat16 [16, 2048, 2048], P('section', 'blk'), parts along dimension 1, may hold values from -6 to 6
- exit_layer: int32 [8192], P('blk'), parts along dimension 0, may hold values from 1 to 4
- lengths: int32 [8192], P('blk'), parts along dimension 0, may hold values from 1 to 16, as said below
- kv_cache: bfloat16 [16, 2048, 16, 256], P('section', 'blk'), parts along dimension 1, may hold values from -256 to 256
- norm_gain: bfloat16 [16, 2048], P('section'), may hold values from 0.5 to 1.5
- w_qkv: bfloat16 [16, 2048, 1280], P('section'), may hold values from -0.0625 to 0.0625
- w_out: bfloat16 [16, 1024, 2048], P('section'), may hold values from -0.1875 to 0.1875
Outputs:
- settled: bfloat16 [8192, 8192], P('blk', 'section'), parts along dimension 0
There are 16 independent parts, one for each index of `blk`. A program takes and returns all parts, laid end to end along the dimension named above; an argument that names none is the same for every part. Nothing has to cross between parts.
Inputs may be any that keep to these rules, and one draw needn't show every extreme that they name: `lengths`: some token has length 16.
All inputs are finite; a program needn't handle non-finite values.
Results may differ from a plain program's by a relative error of at most 0.03.
Values may be sent and summed in bfloat16 or wider, within the bound.
A program may use at most 64 MiB of HBM per device.

v0:
```python
import math

import jax
import jax.numpy as jnp
from jax import lax
from jax.sharding import PartitionSpec as P

BLOCK = 64
MICRO = 8


EPSILON = 1e-05
NEGATIVE = -1e30


def partner(value, axis, distance):
    return lax.ppermute(value, axis, [(i, i ^ 1 << distance) for i in range(lax.axis_size(axis))])


def shifted(value, axis, steps):
    count = lax.axis_size(axis)
    pairs = [(source, (source + steps) % count) for source in range(count)]
    return lax.ppermute(value, axis, pairs)


def body(hidden, exit_layer, lengths, kv_cache, norm_gain, w_qkv, w_out):
    devices = lax.axis_size("section")
    index = lax.axis_index("section")
    shards = max(2, devices // 4)
    cycle_size = devices // shards
    segment_bits = cycle_size.bit_length() - 1
    shard_bits = shards.bit_length() - 1
    segment_index = index // shards
    shard_index = index % shards
    own_blocks = hidden[0]
    gain_row = norm_gain[0].astype(jnp.float32)
    proj_weight = w_qkv[0]
    out_weight = w_out[0]
    cache_all = kv_cache[0]
    query_width = out_weight.shape[0]
    head_size = (proj_weight.shape[1] - query_width) // 2
    heads = query_width // head_size
    quarter = proj_weight.shape[0]
    total_width = quarter * shards
    group_rows = BLOCK // shards
    rounds = MICRO // cycle_size
    context = cache_all.shape[1]
    positions = jnp.arange(context, dtype=jnp.int32)
    blank_block = jnp.zeros((BLOCK, quarter), jnp.bfloat16)

    def advance(carry, microstep):
        incoming, arriving, records = carry
        micro_index = microstep - segment_index
        in_range = (micro_index >= 0) & (micro_index < MICRO)
        slot = jnp.clip(micro_index, 0, MICRO - 1)
        on_turn = microstep % cycle_size == 0
        local_slot = jnp.minimum(microstep // cycle_size, rounds - 1)
        own_block = lax.dynamic_slice_in_dim(own_blocks, local_slot * BLOCK, BLOCK, 0)
        exit_rows = lax.dynamic_slice_in_dim(exit_layer, slot * BLOCK, BLOCK)
        own_lengths = lax.dynamic_slice_in_dim(
            lengths, slot * BLOCK + shard_index * group_rows, group_rows
        )
        own_cache = lax.dynamic_slice_in_dim(cache_all, slot * group_rows, group_rows, 0)
        first_input = jnp.where(on_turn, own_block, arriving)
        entering = jnp.where(segment_index == 0, first_input, incoming)
        active = exit_rows > segment_index
        gate = in_range & (jnp.sum(active.astype(jnp.int32)) > 0)

        def local_partials():
            widened = entering.astype(jnp.float32)
            scaled = (widened * gain_row).astype(jnp.bfloat16)
            return (
                jnp.dot(scaled, proj_weight, preferred_element_type=jnp.float32),
                jnp.sum(widened * widened, axis=1),
            )

        def no_partials():
            return (
                jnp.zeros((BLOCK, proj_weight.shape[1]), jnp.float32),
                jnp.zeros((BLOCK,), jnp.float32),
            )

        partial_proj, partial_squares = lax.cond(gate, local_partials, no_partials)
        kept = (partial_proj, partial_squares)
        for level in range(shard_bits):
            bit = shard_bits - 1 - level
            upper = index >> bit & 1
            halves = tuple(
                (piece.reshape((2, piece.shape[0] // 2) + piece.shape[1:]) for piece in kept)
            )
            keep = tuple((jnp.where(upper == 1, half[1], half[0]) for half in halves))
            send = tuple((jnp.where(upper == 1, half[0], half[1]) for half in halves))
            received = partner(send, "section", bit)
            kept = tuple((first + second for first, second in zip(keep, received)))
        own_proj, own_squares = kept

        def local_attention():
            fitted = own_proj * lax.rsqrt(own_squares / total_width + EPSILON)[:, None]
            query = (fitted[:, :query_width] * (1.0 / math.sqrt(head_size))).astype(jnp.bfloat16)
            query = query.reshape(group_rows, heads, head_size)
            key_new = fitted[:, query_width : query_width + head_size].astype(jnp.bfloat16)
            value_new = fitted[:, query_width + head_size :].astype(jnp.bfloat16)
            scores = jnp.einsum(
                "rhd,rcd->rhc",
                query,
                own_cache[:, :, :head_size],
                preferred_element_type=jnp.float32,
            )
            own = jnp.einsum("rhd,rd->rh", query, key_new, preferred_element_type=jnp.float32)
            usable = (positions[None, :] < own_lengths[:, None])[:, None, :]
            scores = jnp.where(usable, scores, NEGATIVE)
            row_top = jnp.maximum(jnp.max(scores, axis=-1), own)
            raw = jnp.where(usable, jnp.exp(scores - row_top[:, :, None]), jnp.float32(0.0))
            raw_own = jnp.exp(own - row_top)
            total = jnp.sum(raw, axis=-1) + raw_own
            weights = (raw / total[:, :, None]).astype(jnp.bfloat16)
            own_weight = (raw_own / total).astype(jnp.bfloat16)
            attended = jnp.einsum(
                "rhc,rcd->rhd",
                weights,
                own_cache[:, :, head_size:],
                preferred_element_type=jnp.float32,
            )
            attended = (
                attended
                + own_weight.astype(jnp.float32)[:, :, None]
                * value_new.astype(jnp.float32)[:, None, :]
            )
            return attended.astype(jnp.bfloat16).reshape(group_rows, query_width)

        def no_attention():
            return jnp.zeros((group_rows, query_width), jnp.bfloat16)

        collected = lax.cond(gate, local_attention, no_attention)
        for level in range(shard_bits):
            bit = level
            other = partner(collected, "section", bit)
            upper = index >> bit & 1
            collected = jnp.where(
                upper == 1,
                jnp.concatenate([other, collected], 0),
                jnp.concatenate([collected, other], 0),
            )

        def local_update():
            branch_out = jnp.dot(collected, out_weight, preferred_element_type=jnp.float32)
            updated = (entering.astype(jnp.float32) + branch_out).astype(jnp.bfloat16)
            return jnp.where(active[:, None], updated, entering)

        def keep_state():
            return entering

        outgoing = lax.cond(gate, local_update, keep_state)
        leaving = in_range & (exit_rows == segment_index + 1)
        previous = lax.dynamic_slice_in_dim(records, slot * BLOCK, BLOCK, 0)
        records = lax.dynamic_update_slice_in_dim(
            records, jnp.where(leaving[:, None], outgoing, previous), slot * BLOCK, 0
        )
        relayed = jnp.where(on_turn & (segment_index > 0), own_block, arriving)
        incoming, arriving = shifted((outgoing, relayed), "section", shards)
        return ((incoming, arriving, records), None)

    start = (blank_block, blank_block, jnp.zeros((MICRO * BLOCK, quarter), jnp.bfloat16))
    carry, _ = lax.scan(advance, start, jnp.arange(MICRO + cycle_size - 1, dtype=jnp.int32))
    kept = carry[2]
    for level in range(segment_bits):
        bit = shard_bits + segment_bits - 1 - level
        upper = index >> bit & 1
        halves = kept.reshape(kept.shape[0], 2, kept.shape[1] // 2)
        keep = jnp.where(upper == 1, halves[:, 1], halves[:, 0])
        send = jnp.where(upper == 1, halves[:, 0], halves[:, 1])
        received = partner(send, "section", bit)
        kept = (keep.astype(jnp.float32) + received.astype(jnp.float32)).astype(jnp.bfloat16)
    return kept


def solution(mesh):
    return jax.shard_map(
        body,
        mesh=mesh,
        in_specs=(
            P("section", "blk", None),
            P("blk"),
            P("blk"),
            P("section", "blk", None, None),
            P("section", None),
            P("section", None, None),
            P("section", None, None),
        ),
        out_specs=P("blk", "section"),
        check_vma=False,
    )
```

profile of v0, /device:TPU:32, one launch (start us, length us, event | category | flops | bytes accessed | tf_op | source)
XLA Modules:
  0.0 571.9 jit_solution(7820778162144231576)
XLA Ops:
  1.1 537.8 %while.17 = (s32[]{:T(128)}, bf16[64,2048]{1,0:T(8,128)(2,1)S(1)}, bf16[64,2048]{1,0:T(8,128)(2,1)S(1)}, bf16[512,2048]{1,0:T(8,128)(2,1)S(1)}, s32[11]{0:T(128)...) while((s32[]{:T(128)}, bf16[64,2048]{1,0:T(8,128)(2,1)S(1)}, ...), condition=%wide.region_11.12_spmd.clone, body=%wide.region_0.11_spmd.clone.sunk | while | flops 608109760 | bytes 20330868 | solution.py:164
  7.8 3.8 conditional.9
  7.8 3.5 fusion.4
  16.7 5.2 collective-permute-done
  26.6 3.5 conditional.10
  36.0 4.1 collective-permute-done.5
  43.5 7.4 %collective-permute-done.6 = bf16[64,2048]{1,0:T(8,128)(2,1)S(1)} collective-permute-done((bf16[64,2048]{1,0:T(8,128)(2,1)S(1)}, bf16[64,2048]{1,0:T(8,128)(2,1)S(1)}, u32[]{:S(2)}, u32[]{:S(2)}) %collective-permute-start.6) | collective-permute-done | bytes 262176 | tf_op jit(solution)/shard_map/while/body/eval_jaxpr/ppermute | solution.py:23
  57.6 3.8 conditional.9
  57.7 3.5 fusion.4
  66.5 3.4 collective-permute-done
  74.7 3.5 conditional.10
  91.4 7.4 %collective-permute-done.6 = bf16[64,2048]{1,0:T(8,128)(2,1)S(1)} collective-permute-done((bf16[64,2048]{1,0:T(8,128)(2,1)S(1)}, bf16[64,2048]{1,0:T(8,128)(2,1)S(1)}, u32[]{:S(2)}, u32[]{:S(2)}) %collective-permute-start.6) | collective-permute-done | bytes 262176 | tf_op jit(solution)/shard_map/while/body/eval_jaxpr/ppermute | solution.py:23
  105.6 3.8 conditional.9
  105.6 3.5 fusion.4
  114.5 5.2 collective-permute-done
  124.4 3.5 conditional.10
  133.2 4.6 collective-permute-done.5
  141.2 7.4 %collective-permute-done.6 = bf16[64,2048]{1,0:T(8,128)(2,1)S(1)} collective-permute-done((bf16[64,2048]{1,0:T(8,128)(2,1)S(1)}, bf16[64,2048]{1,0:T(8,128)(2,1)S(1)}, u32[]{:S(2)}, u32[]{:S(2)}) %collective-permute-start.6) | collective-permute-done | bytes 262176 | tf_op jit(solution)/shard_map/while/body/eval_jaxpr/ppermute | solution.py:23
  155.3 3.8 conditional.9
  155.3 3.5 fusion.4
  172.0 3.5 conditional.10
  179.5 3.3 collective-permute-start.5
  188.7 7.4 %collective-permute-done.6 = bf16[64,2048]{1,0:T(8,128)(2,1)S(1)} collective-permute-done((bf16[64,2048]{1,0:T(8,128)(2,1)S(1)}, bf16[64,2048]{1,0:T(8,128)(2,1)S(1)}, u32[]{:S(2)}, u32[]{:S(2)}) %collective-permute-start.6) | collective-permute-done | bytes 262176 | tf_op jit(solution)/shard_map/while/body/eval_jaxpr/ppermute | solution.py:23
  202.8 3.8 conditional.9
  202.9 3.5 fusion.4
  206.6 3.2 collective-permute-start.2
  211.7 5.1 collective-permute-done
  221.5 3.5 conditional.10
  230.3 4.8 collective-permute-done.5
  238.5 7.4 %collective-permute-done.6 = bf16[64,2048]{1,0:T(8,128)(2,1)S(1)} collective-permute-done((bf16[64,2048]{1,0:T(8,128)(2,1)S(1)}, bf16[64,2048]{1,0:T(8,128)(2,1)S(1)}, u32[]{:S(2)}, u32[]{:S(2)}) %collective-permute-start.6) | collective-permute-done | bytes 262176 | tf_op jit(solution)/shard_map/while/body/eval_jaxpr/ppermute | solution.py:23
  252.6 3.8 conditional.9
  252.6 3.5 fusion.4
  261.5 3.2 collective-permute-done
  269.5 3.5 conditional.10
  277.3 3.2 collective-permute-start.5
  286.6 8.8 %collective-permute-done.6 = bf16[64,2048]{1,0:T(8,128)(2,1)S(1)} collective-permute-done((bf16[64,2048]{1,0:T(8,128)(2,1)S(1)}, bf16[64,2048]{1,0:T(8,128)(2,1)S(1)}, u32[]{:S(2)}, u32[]{:S(2)}) %collective-permute-start.6) | collective-permute-done | bytes 262176 | tf_op jit(solution)/shard_map/while/body/eval_jaxpr/ppermute | solution.py:23
  302.1 3.8 conditional.9
  302.1 3.5 fusion.4
  305.8 3.7 collective-permute-start.2
  311.1 5.4 collective-permute-done
  321.2 3.5 conditional.10
  329.5 5.1 collective-permute-done.5
  338.0 8.4 %collective-permute-done.6 = bf16[64,2048]{1,0:T(8,128)(2,1)S(1)} collective-permute-done((bf16[64,2048]{1,0:T(8,128)(2,1)S(1)}, bf16[64,2048]{1,0:T(8,128)(2,1)S(1)}, u32[]{:S(2)}, u32[]{:S(2)}) %collective-permute-start.6) | collective-permute-done | bytes 262176 | tf_op jit(solution)/shard_map/while/body/eval_jaxpr/ppermute | solution.py:23
  353.1 3.8 conditional.9
  353.1 3.5 fusion.4
  369.7 3.5 conditional.10
  377.2 4.6 collective-permute-start.5
  387.4 7.4 %collective-permute-done.6 = bf16[64,2048]{1,0:T(8,128)(2,1)S(1)} collective-permute-done((bf16[64,2048]{1,0:T(8,128)(2,1)S(1)}, bf16[64,2048]{1,0:T(8,128)(2,1)S(1)}, u32[]{:S(2)}, u32[]{:S(2)}) %collective-permute-start.6) | collective-permute-done | bytes 262176 | tf_op jit(solution)/shard_map/while/body/eval_jaxpr/ppermute | solution.py:23
  401.6 3.6 collective-permute-start.2
  406.8 5.4 collective-permute-done
  418.2 5.9 %collective-permute-start.7 = (bf16[64,2048]{1,0:T(8,128)(2,1)S(1)}, bf16[64,2048]{1,0:T(8,128)(2,1)S(1)}, u32[]{:S(2)}, u32[]{:S(2)}) collective-permute-start(bf16[64,2048]{1,0:T(8,128)(2,1)S(1)} %get-tuple-element.698), channel_id=1, source_target_pairs={{0,4},{1,5},{2,6},{3,7},{4,8},{5,9},{6,10},{7,11},{8,12},{9,13},{1... | collective-permute-start | bytes 786440 | tf_op jit(solution)/shard_map/while/body/eval_jaxpr/ppermute | solution.py:23
  424.6 5.4 collective-permute-done.5
  430.0 6.0 %collective-permute-start.6 = (bf16[64,2048]{1,0:T(8,128)(2,1)S(1)}, bf16[64,2048]{1,0:T(8,128)(2,1)S(1)}, u32[]{:S(2)}, u32[]{:S(2)}) collective-permute-start(bf16[64,2048]{1,0:T(8,128)(2,1)S(1)} %get-tuple-element.798), channel_id=1, source_target_pairs={{0,4},{1,5},{2,6},{3,7},{4,8},{5,9},{6,10},{7,11},{8,12},{9,13},{1... | collective-permute-start | bytes 786440 | tf_op jit(solution)/shard_map/while/body/eval_jaxpr/ppermute | solution.py:23
  436.1 5.2 collective-permute-done.6
  464.8 3.3 collective-permute-start.5
  470.7 5.1 collective-permute-start.6
  476.0 15.8 %collective-permute-done.6 = bf16[64,2048]{1,0:T(8,128)(2,1)S(1)} collective-permute-done((bf16[64,2048]{1,0:T(8,128)(2,1)S(1)}, bf16[64,2048]{1,0:T(8,128)(2,1)S(1)}, u32[]{:S(2)}, u32[]{:S(2)}) %collective-permute-start.6) | collective-permute-done | bytes 262176 | tf_op jit(solution)/shard_map/while/body/eval_jaxpr/ppermute | solution.py:23
  498.6 3.5 collective-permute-start.2
  503.8 5.2 collective-permute-done
  515.0 3.5 collective-permute-start.7
  519.2 5.2 collective-permute-done.5
  527.4 11.4 %collective-permute-done.6 = bf16[64,2048]{1,0:T(8,128)(2,1)S(1)} collective-permute-done((bf16[64,2048]{1,0:T(8,128)(2,1)S(1)}, bf16[64,2048]{1,0:T(8,128)(2,1)S(1)}, u32[]{:S(2)}, u32[]{:S(2)}) %collective-permute-start.6) | collective-permute-done | bytes 262176 | tf_op jit(solution)/shard_map/while/body/eval_jaxpr/ppermute | solution.py:23
  544.3 15.4 %collective-permute-done.8 = bf16[512,1024]{0,1:T(8,128)(2,1)} collective-permute-done((bf16[512,1024]{0,1:T(8,128)(2,1)S(1)}, bf16[512,1024]{0,1:T(8,128)(2,1)}, u32[]{:S(2)}, u32[]{:S(2)}) %collective-permute-start.8) | collective-permute-done | bytes 1048608 | tf_op jit(solution)/shard_map/ppermute | solution.py:17
  561.5 9.2 %collective-permute-done.9 = bf16[512,512]{0,1:T(8,128)(2,1)S(1)} collective-permute-done((bf16[512,512]{0,1:T(8,128)(2,1)S(1)}, bf16[512,512]{0,1:T(8,128)(2,1)S(1)}, u32[]{:S(2)}, u32[]{:S(2)}) %collective-permute-start.9) | collective-permute-done | bytes 524320 | tf_op jit(solution)/shard_map/ppermute | solution.py:17
  (508 shorter events, 285.5 us)
Async XLA Ops:
  11.6 5.1 collective-permute-start.2
  14.7 7.3 %collective-permute-start = (f32[32,1280]{1,0:T(8,128)S(1)}, f32[32,1280]{1,0:T(8,128)S(1)}, u32[]{:S(2)}, u32[]{:S(2)}) collective-permute-start(f32[32,1280]{1,0:T(8,128)S(1)} %broadcast_select_fusion.12), channel_id=1, source_target_pairs={{0,2},{1,3},{2,0},{3,1},{4,6},{5,7},{6,4},{7,5},{8,10},{9,11},{10,... | collective-permute-start | bytes 491528 | tf_op jit(solution)/shard_map/while/body/eval_jaxpr/ppermute | solution.py:17
  31.4 12.1 %collective-permute-start.7 = (bf16[64,2048]{1,0:T(8,128)(2,1)S(1)}, bf16[64,2048]{1,0:T(8,128)(2,1)S(1)}, u32[]{:S(2)}, u32[]{:S(2)}) collective-permute-start(bf16[64,2048]{1,0:T(8,128)(2,1)S(1)} %get-tuple-element.698), channel_id=1, source_target_pairs={{0,4},{1,5},{2,6},{3,7},{4,8},{5,9},{6,10},{7,11},{8,12},{9,13},{1... | collective-permute-start | bytes 786440 | tf_op jit(solution)/shard_map/while/body/eval_jaxpr/ppermute | solution.py:23
  34.3 5.9 %collective-permute-start.5 = (bf16[32,1024]{1,0:T(8,128)(2,1)S(1)}, bf16[32,1024]{1,0:T(8,128)(2,1)S(1)}, u32[]{:S(2)}, u32[]{:S(2)}) collective-permute-start(bf16[32,1024]{1,0:T(8,128)(2,1)S(1)} %maximum_select_fusion.2), channel_id=1, source_target_pairs={{0,2},{1,3},{2,0},{3,1},{4,6},{5,7},{6,4},{7,5},{8,10},{9,11},{10,... | collective-permute-start | bytes 196616 | tf_op jit(solution)/shard_map/while/body/eval_jaxpr/ppermute | solution.py:17
  43.3 7.7 %collective-permute-start.6 = (bf16[64,2048]{1,0:T(8,128)(2,1)S(1)}, bf16[64,2048]{1,0:T(8,128)(2,1)S(1)}, u32[]{:S(2)}, u32[]{:S(2)}) collective-permute-start(bf16[64,2048]{1,0:T(8,128)(2,1)S(1)} %get-tuple-element.798), channel_id=1, source_target_pairs={{0,4},{1,5},{2,6},{3,7},{4,8},{5,9},{6,10},{7,11},{8,12},{9,13},{1... | collective-permute-start | bytes 786440 | tf_op jit(solution)/shard_map/while/body/eval_jaxpr/ppermute | solution.py:23
  61.4 5.1 collective-permute-start.2
  63.1 6.9 %collective-permute-start = (f32[32,1280]{1,0:T(8,128)S(1)}, f32[32,1280]{1,0:T(8,128)S(1)}, u32[]{:S(2)}, u32[]{:S(2)}) collective-permute-start(f32[32,1280]{1,0:T(8,128)S(1)} %broadcast_select_fusion.12), channel_id=1, source_target_pairs={{0,2},{1,3},{2,0},{3,1},{4,6},{5,7},{6,4},{7,5},{8,10},{9,11},{10,... | collective-permute-start | bytes 491528 | tf_op jit(solution)/shard_map/while/body/eval_jaxpr/ppermute | solution.py:17
  70.0 4.6 collective-permute-start.1
  79.4 12.0 %collective-permute-start.7 = (bf16[64,2048]{1,0:T(8,128)(2,1)S(1)}, bf16[64,2048]{1,0:T(8,128)(2,1)S(1)}, u32[]{:S(2)}, u32[]{:S(2)}) collective-permute-start(bf16[64,2048]{1,0:T(8,128)(2,1)S(1)} %get-tuple-element.698), channel_id=1, source_target_pairs={{0,4},{1,5},{2,6},{3,7},{4,8},{5,9},{6,10},{7,11},{8,12},{9,13},{1... | collective-permute-start | bytes 786440 | tf_op jit(solution)/shard_map/while/body/eval_jaxpr/ppermute | solution.py:23
  82.2 5.9 %collective-permute-start.5 = (bf16[32,1024]{1,0:T(8,128)(2,1)S(1)}, bf16[32,1024]{1,0:T(8,128)(2,1)S(1)}, u32[]{:S(2)}, u32[]{:S(2)}) collective-permute-start(bf16[32,1024]{1,0:T(8,128)(2,1)S(1)} %maximum_select_fusion.2), channel_id=1, source_target_pairs={{0,2},{1,3},{2,0},{3,1},{4,6},{5,7},{6,4},{7,5},{8,10},{9,11},{10,... | collective-permute-start | bytes 196616 | tf_op jit(solution)/shard_map/while/body/eval_jaxpr/ppermute | solution.py:17
  91.2 7.7 %collective-permute-start.6 = (bf16[64,2048]{1,0:T(8,128)(2,1)S(1)}, bf16[64,2048]{1,0:T(8,128)(2,1)S(1)}, u32[]{:S(2)}, u32[]{:S(2)}) collective-permute-start(bf16[64,2048]{1,0:T(8,128)(2,1)S(1)} %get-tuple-element.798), channel_id=1, source_target_pairs={{0,4},{1,5},{2,6},{3,7},{4,8},{5,9},{6,10},{7,11},{8,12},{9,13},{1... | collective-permute-start | bytes 786440 | tf_op jit(solution)/shard_map/while/body/eval_jaxpr/ppermute | solution.py:23
  109.4 5.1 collective-permute-start.2
  112.4 7.3 %collective-permute-start = (f32[32,1280]{1,0:T(8,128)S(1)}, f32[32,1280]{1,0:T(8,128)S(1)}, u32[]{:S(2)}, u32[]{:S(2)}) collective-permute-start(f32[32,1280]{1,0:T(8,128)S(1)} %broadcast_select_fusion.12), channel_id=1, source_target_pairs={{0,2},{1,3},{2,0},{3,1},{4,6},{5,7},{6,4},{7,5},{8,10},{9,11},{10,... | collective-permute-start | bytes 491528 | tf_op jit(solution)/shard_map/while/body/eval_jaxpr/ppermute | solution.py:17
  129.1 12.0 %collective-permute-start.7 = (bf16[64,2048]{1,0:T(8,128)(2,1)S(1)}, bf16[64,2048]{1,0:T(8,128)(2,1)S(1)}, u32[]{:S(2)}, u32[]{:S(2)}) collective-permute-start(bf16[64,2048]{1,0:T(8,128)(2,1)S(1)} %get-tuple-element.698), channel_id=1, source_target_pairs={{0,4},{1,5},{2,6},{3,7},{4,8},{5,9},{6,10},{7,11},{8,12},{9,13},{1... | collective-permute-start | bytes 786440 | tf_op jit(solution)/shard_map/while/body/eval_jaxpr/ppermute | solution.py:23
  131.9 5.9 %collective-permute-start.5 = (bf16[32,1024]{1,0:T(8,128)(2,1)S(1)}, bf16[32,1024]{1,0:T(8,128)(2,1)S(1)}, u32[]{:S(2)}, u32[]{:S(2)}) collective-permute-start(bf16[32,1024]{1,0:T(8,128)(2,1)S(1)} %maximum_select_fusion.2), channel_id=1, source_target_pairs={{0,2},{1,3},{2,0},{3,1},{4,6},{5,7},{6,4},{7,5},{8,10},{9,11},{10,... | collective-permute-start | bytes 196616 | tf_op jit(solution)/shard_map/while/body/eval_jaxpr/ppermute | solution.py:17
  140.9 7.7 %collective-permute-start.6 = (bf16[64,2048]{1,0:T(8,128)(2,1)S(1)}, bf16[64,2048]{1,0:T(8,128)(2,1)S(1)}, u32[]{:S(2)}, u32[]{:S(2)}) collective-permute-start(bf16[64,2048]{1,0:T(8,128)(2,1)S(1)} %get-tuple-element.798), channel_id=1, source_target_pairs={{0,4},{1,5},{2,6},{3,7},{4,8},{5,9},{6,10},{7,11},{8,12},{9,13},{1... | collective-permute-start | bytes 786440 | tf_op jit(solution)/shard_map/while/body/eval_jaxpr/ppermute | solution.py:23
  159.1 5.1 collective-permute-start.2
  160.2 6.9 %collective-permute-start = (f32[32,1280]{1,0:T(8,128)S(1)}, f32[32,1280]{1,0:T(8,128)S(1)}, u32[]{:S(2)}, u32[]{:S(2)}) collective-permute-start(f32[32,1280]{1,0:T(8,128)S(1)} %broadcast_select_fusion.12), channel_id=1, source_target_pairs={{0,2},{1,3},{2,0},{3,1},{4,6},{5,7},{6,4},{7,5},{8,10},{9,11},{10,... | collective-permute-start | bytes 491528 | tf_op jit(solution)/shard_map/while/body/eval_jaxpr/ppermute | solution.py:17
  167.2 4.7 collective-permute-start.1
  176.6 12.1 %collective-permute-start.7 = (bf16[64,2048]{1,0:T(8,128)(2,1)S(1)}, bf16[64,2048]{1,0:T(8,128)(2,1)S(1)}, u32[]{:S(2)}, u32[]{:S(2)}) collective-permute-start(bf16[64,2048]{1,0:T(8,128)(2,1)S(1)} %get-tuple-element.698), channel_id=1, source_target_pairs={{0,4},{1,5},{2,6},{3,7},{4,8},{5,9},{6,10},{7,11},{8,12},{9,13},{1... | collective-permute-start | bytes 786440 | tf_op jit(solution)/shard_map/while/body/eval_jaxpr/ppermute | solution.py:23
  179.5 5.9 %collective-permute-start.5 = (bf16[32,1024]{1,0:T(8,128)(2,1)S(1)}, bf16[32,1024]{1,0:T(8,128)(2,1)S(1)}, u32[]{:S(2)}, u32[]{:S(2)}) collective-permute-start(bf16[32,1024]{1,0:T(8,128)(2,1)S(1)} %maximum_select_fusion.2), channel_id=1, source_target_pairs={{0,2},{1,3},{2,0},{3,1},{4,6},{5,7},{6,4},{7,5},{8,10},{9,11},{10,... | collective-permute-start | bytes 196616 | tf_op jit(solution)/shard_map/while/body/eval_jaxpr/ppermute | solution.py:17
  188.5 7.7 %collective-permute-start.6 = (bf16[64,2048]{1,0:T(8,128)(2,1)S(1)}, bf16[64,2048]{1,0:T(8,128)(2,1)S(1)}, u32[]{:S(2)}, u32[]{:S(2)}) collective-permute-start(bf16[64,2048]{1,0:T(8,128)(2,1)S(1)} %get-tuple-element.798), channel_id=1, source_target_pairs={{0,4},{1,5},{2,6},{3,7},{4,8},{5,9},{6,10},{7,11},{8,12},{9,13},{1... | collective-permute-start | bytes 786440 | tf_op jit(solution)/shard_map/while/body/eval_jaxpr/ppermute | solution.py:23
  206.6 5.1 collective-permute-start.2
  209.9 6.9 %collective-permute-start = (f32[32,1280]{1,0:T(8,128)S(1)}, f32[32,1280]{1,0:T(8,128)S(1)}, u32[]{:S(2)}, u32[]{:S(2)}) collective-permute-start(f32[32,1280]{1,0:T(8,128)S(1)} %broadcast_select_fusion.12), channel_id=1, source_target_pairs={{0,2},{1,3},{2,0},{3,1},{4,6},{5,7},{6,4},{7,5},{8,10},{9,11},{10,... | collective-permute-start | bytes 491528 | tf_op jit(solution)/shard_map/while/body/eval_jaxpr/ppermute | solution.py:17
  216.9 4.6 collective-permute-start.1
  226.2 12.2 %collective-permute-start.7 = (bf16[64,2048]{1,0:T(8,128)(2,1)S(1)}, bf16[64,2048]{1,0:T(8,128)(2,1)S(1)}, u32[]{:S(2)}, u32[]{:S(2)}) collective-permute-start(bf16[64,2048]{1,0:T(8,128)(2,1)S(1)} %get-tuple-element.698), channel_id=1, source_target_pairs={{0,4},{1,5},{2,6},{3,7},{4,8},{5,9},{6,10},{7,11},{8,12},{9,13},{1... | collective-permute-start | bytes 786440 | tf_op jit(solution)/shard_map/while/body/eval_jaxpr/ppermute | solution.py:23
  229.0 6.1 %collective-permute-start.5 = (bf16[32,1024]{1,0:T(8,128)(2,1)S(1)}, bf16[32,1024]{1,0:T(8,128)(2,1)S(1)}, u32[]{:S(2)}, u32[]{:S(2)}) collective-permute-start(bf16[32,1024]{1,0:T(8,128)(2,1)S(1)} %maximum_select_fusion.2), channel_id=1, source_target_pairs={{0,2},{1,3},{2,0},{3,1},{4,6},{5,7},{6,4},{7,5},{8,10},{9,11},{10,... | collective-permute-start | bytes 196616 | tf_op jit(solution)/shard_map/while/body/eval_jaxpr/ppermute | solution.py:17
  238.2 7.7 %collective-permute-start.6 = (bf16[64,2048]{1,0:T(8,128)(2,1)S(1)}, bf16[64,2048]{1,0:T(8,128)(2,1)S(1)}, u32[]{:S(2)}, u32[]{:S(2)}) collective-permute-start(bf16[64,2048]{1,0:T(8,128)(2,1)S(1)} %get-tuple-element.798), channel_id=1, source_target_pairs={{0,4},{1,5},{2,6},{3,7},{4,8},{5,9},{6,10},{7,11},{8,12},{9,13},{1... | collective-permute-start | bytes 786440 | tf_op jit(solution)/shard_map/while/body/eval_jaxpr/ppermute | solution.py:23
  256.4 5.1 collective-permute-start.2
  257.8 6.9 %collective-permute-start = (f32[32,1280]{1,0:T(8,128)S(1)}, f32[32,1280]{1,0:T(8,128)S(1)}, u32[]{:S(2)}, u32[]{:S(2)}) collective-permute-start(f32[32,1280]{1,0:T(8,128)S(1)} %broadcast_select_fusion.12), channel_id=1, source_target_pairs={{0,2},{1,3},{2,0},{3,1},{4,6},{5,7},{6,4},{7,5},{8,10},{9,11},{10,... | collective-permute-start | bytes 491528 | tf_op jit(solution)/shard_map/while/body/eval_jaxpr/ppermute | solution.py:17
  264.8 4.6 collective-permute-start.1
  274.2 12.4 %collective-permute-start.7 = (bf16[64,2048]{1,0:T(8,128)(2,1)S(1)}, bf16[64,2048]{1,0:T(8,128)(2,1)S(1)}, u32[]{:S(2)}, u32[]{:S(2)}) collective-permute-start(bf16[64,2048]{1,0:T(8,128)(2,1)S(1)} %get-tuple-element.698), channel_id=1, source_target_pairs={{0,4},{1,5},{2,6},{3,7},{4,8},{5,9},{6,10},{7,11},{8,12},{9,13},{1... | collective-permute-start | bytes 786440 | tf_op jit(solution)/shard_map/while/body/eval_jaxpr/ppermute | solution.py:23
  277.3 5.9 %collective-permute-start.5 = (bf16[32,1024]{1,0:T(8,128)(2,1)S(1)}, bf16[32,1024]{1,0:T(8,128)(2,1)S(1)}, u32[]{:S(2)}, u32[]{:S(2)}) collective-permute-start(bf16[32,1024]{1,0:T(8,128)(2,1)S(1)} %maximum_select_fusion.2), channel_id=1, source_target_pairs={{0,2},{1,3},{2,0},{3,1},{4,6},{5,7},{6,4},{7,5},{8,10},{9,11},{10,... | collective-permute-start | bytes 196616 | tf_op jit(solution)/shard_map/while/body/eval_jaxpr/ppermute | solution.py:17
  286.3 9.0 %collective-permute-start.6 = (bf16[64,2048]{1,0:T(8,128)(2,1)S(1)}, bf16[64,2048]{1,0:T(8,128)(2,1)S(1)}, u32[]{:S(2)}, u32[]{:S(2)}) collective-permute-start(bf16[64,2048]{1,0:T(8,128)(2,1)S(1)} %get-tuple-element.798), channel_id=1, source_target_pairs={{0,4},{1,5},{2,6},{3,7},{4,8},{5,9},{6,10},{7,11},{8,12},{9,13},{1... | collective-permute-start | bytes 786440 | tf_op jit(solution)/shard_map/while/body/eval_jaxpr/ppermute | solution.py:23
  305.8 5.3 collective-permute-start.2
  309.6 6.9 %collective-permute-start = (f32[32,1280]{1,0:T(8,128)S(1)}, f32[32,1280]{1,0:T(8,128)S(1)}, u32[]{:S(2)}, u32[]{:S(2)}) collective-permute-start(f32[32,1280]{1,0:T(8,128)S(1)} %broadcast_select_fusion.12), channel_id=1, source_target_pairs={{0,2},{1,3},{2,0},{3,1},{4,6},{5,7},{6,4},{7,5},{8,10},{9,11},{10,... | collective-permute-start | bytes 491528 | tf_op jit(solution)/shard_map/while/body/eval_jaxpr/ppermute | solution.py:17
  325.9 12.0 %collective-permute-start.7 = (bf16[64,2048]{1,0:T(8,128)(2,1)S(1)}, bf16[64,2048]{1,0:T(8,128)(2,1)S(1)}, u32[]{:S(2)}, u32[]{:S(2)}) collective-permute-start(bf16[64,2048]{1,0:T(8,128)(2,1)S(1)} %get-tuple-element.698), channel_id=1, source_target_pairs={{0,4},{1,5},{2,6},{3,7},{4,8},{5,9},{6,10},{7,11},{8,12},{9,13},{1... | collective-permute-start | bytes 786440 | tf_op jit(solution)/shard_map/while/body/eval_jaxpr/ppermute | solution.py:23
  328.7 5.9 %collective-permute-start.5 = (bf16[32,1024]{1,0:T(8,128)(2,1)S(1)}, bf16[32,1024]{1,0:T(8,128)(2,1)S(1)}, u32[]{:S(2)}, u32[]{:S(2)}) collective-permute-start(bf16[32,1024]{1,0:T(8,128)(2,1)S(1)} %maximum_select_fusion.2), channel_id=1, source_target_pairs={{0,2},{1,3},{2,0},{3,1},{4,6},{5,7},{6,4},{7,5},{8,10},{9,11},{10,... | collective-permute-start | bytes 196616 | tf_op jit(solution)/shard_map/while/body/eval_jaxpr/ppermute | solution.py:17
  337.7 8.6 %collective-permute-start.6 = (bf16[64,2048]{1,0:T(8,128)(2,1)S(1)}, bf16[64,2048]{1,0:T(8,128)(2,1)S(1)}, u32[]{:S(2)}, u32[]{:S(2)}) collective-permute-start(bf16[64,2048]{1,0:T(8,128)(2,1)S(1)} %get-tuple-element.798), channel_id=1, source_target_pairs={{0,4},{1,5},{2,6},{3,7},{4,8},{5,9},{6,10},{7,11},{8,12},{9,13},{1... | collective-permute-start | bytes 786440 | tf_op jit(solution)/shard_map/while/body/eval_jaxpr/ppermute | solution.py:23
  356.9 5.1 collective-permute-start.2
  357.7 6.9 %collective-permute-start = (f32[32,1280]{1,0:T(8,128)S(1)}, f32[32,1280]{1,0:T(8,128)S(1)}, u32[]{:S(2)}, u32[]{:S(2)}) collective-permute-start(f32[32,1280]{1,0:T(8,128)S(1)} %broadcast_select_fusion.12), channel_id=1, source_target_pairs={{0,2},{1,3},{2,0},{3,1},{4,6},{5,7},{6,4},{7,5},{8,10},{9,11},{10,... | collective-permute-start | bytes 491528 | tf_op jit(solution)/shard_map/while/body/eval_jaxpr/ppermute | solution.py:17
  364.7 5.0 collective-permute-start.1
  374.1 13.3 %collective-permute-start.7 = (bf16[64,2048]{1,0:T(8,128)(2,1)S(1)}, bf16[64,2048]{1,0:T(8,128)(2,1)S(1)}, u32[]{:S(2)}, u32[]{:S(2)}) collective-permute-start(bf16[64,2048]{1,0:T(8,128)(2,1)S(1)} %get-tuple-element.698), channel_id=1, source_target_pairs={{0,4},{1,5},{2,6},{3,7},{4,8},{5,9},{6,10},{7,11},{8,12},{9,13},{1... | collective-permute-start | bytes 786440 | tf_op jit(solution)/shard_map/while/body/eval_jaxpr/ppermute | solution.py:23
  377.2 6.8 %collective-permute-start.5 = (bf16[32,1024]{1,0:T(8,128)(2,1)S(1)}, bf16[32,1024]{1,0:T(8,128)(2,1)S(1)}, u32[]{:S(2)}, u32[]{:S(2)}) collective-permute-start(bf16[32,1024]{1,0:T(8,128)(2,1)S(1)} %maximum_select_fusion.2), channel_id=1, source_target_pairs={{0,2},{1,3},{2,0},{3,1},{4,6},{5,7},{6,4},{7,5},{8,10},{9,11},{10,... | collective-permute-start | bytes 196616 | tf_op jit(solution)/shard_map/while/body/eval_jaxpr/ppermute | solution.py:17
  387.2 7.7 %collective-permute-start.6 = (bf16[64,2048]{1,0:T(8,128)(2,1)S(1)}, bf16[64,2048]{1,0:T(8,128)(2,1)S(1)}, u32[]{:S(2)}, u32[]{:S(2)}) collective-permute-start(bf16[64,2048]{1,0:T(8,128)(2,1)S(1)} %get-tuple-element.798), channel_id=1, source_target_pairs={{0,4},{1,5},{2,6},{3,7},{4,8},{5,9},{6,10},{7,11},{8,12},{9,13},{1... | collective-permute-start | bytes 786440 | tf_op jit(solution)/shard_map/while/body/eval_jaxpr/ppermute | solution.py:23
  401.6 5.2 collective-permute-start.2
  405.3 6.9 %collective-permute-start = (f32[32,1280]{1,0:T(8,128)S(1)}, f32[32,1280]{1,0:T(8,128)S(1)}, u32[]{:S(2)}, u32[]{:S(2)}) collective-permute-start(f32[32,1280]{1,0:T(8,128)S(1)} %broadcast_select_fusion.12), channel_id=1, source_target_pairs={{0,2},{1,3},{2,0},{3,1},{4,6},{5,7},{6,4},{7,5},{8,10},{9,11},{10,... | collective-permute-start | bytes 491528 | tf_op jit(solution)/shard_map/while/body/eval_jaxpr/ppermute | solution.py:17
  416.9 7.1 %collective-permute-start.4 = (bf16[16,1024]{1,0:T(8,128)(2,1)S(1)}, bf16[16,1024]{1,0:T(8,128)(2,1)S(1)}, u32[]{:S(2)}, u32[]{:S(2)}) collective-permute-start(bf16[16,1024]{1,0:T(8,128)(2,1)S(1)} %get-tuple-element.797), channel_id=1, source_target_pairs={{0,1},{1,0},{2,3},{3,2},{4,5},{5,4},{6,7},{7,6},{8,9},{9,8},{10,11... | collective-permute-start | bytes 98312 | tf_op jit(solution)/shard_map/while/body/eval_jaxpr/ppermute | solution.py:17
  418.2 18.0 %collective-permute-start.7 = (bf16[64,2048]{1,0:T(8,128)(2,1)S(1)}, bf16[64,2048]{1,0:T(8,128)(2,1)S(1)}, u32[]{:S(2)}, u32[]{:S(2)}) collective-permute-start(bf16[64,2048]{1,0:T(8,128)(2,1)S(1)} %get-tuple-element.698), channel_id=1, source_target_pairs={{0,4},{1,5},{2,6},{3,7},{4,8},{5,9},{6,10},{7,11},{8,12},{9,13},{1... | collective-permute-start | bytes 786440 | tf_op jit(solution)/shard_map/while/body/eval_jaxpr/ppermute | solution.py:23
  424.1 5.9 %collective-permute-start.5 = (bf16[32,1024]{1,0:T(8,128)(2,1)S(1)}, bf16[32,1024]{1,0:T(8,128)(2,1)S(1)}, u32[]{:S(2)}, u32[]{:S(2)}) collective-permute-start(bf16[32,1024]{1,0:T(8,128)(2,1)S(1)} %maximum_select_fusion.2), channel_id=1, source_target_pairs={{0,2},{1,3},{2,0},{3,1},{4,6},{5,7},{6,4},{7,5},{8,10},{9,11},{10,... | collective-permute-start | bytes 196616 | tf_op jit(solution)/shard_map/while/body/eval_jaxpr/ppermute | solution.py:17
  430.0 11.4 %collective-permute-start.6 = (bf16[64,2048]{1,0:T(8,128)(2,1)S(1)}, bf16[64,2048]{1,0:T(8,128)(2,1)S(1)}, u32[]{:S(2)}, u32[]{:S(2)}) collective-permute-start(bf16[64,2048]{1,0:T(8,128)(2,1)S(1)} %get-tuple-element.798), channel_id=1, source_target_pairs={{0,4},{1,5},{2,6},{3,7},{4,8},{5,9},{6,10},{7,11},{8,12},{9,13},{1... | collective-permute-start | bytes 786440 | tf_op jit(solution)/shard_map/while/body/eval_jaxpr/ppermute | solution.py:23
  448.2 5.2 collective-permute-start.2
  448.8 7.2 %collective-permute-start = (f32[32,1280]{1,0:T(8,128)S(1)}, f32[32,1280]{1,0:T(8,128)S(1)}, u32[]{:S(2)}, u32[]{:S(2)}) collective-permute-start(f32[32,1280]{1,0:T(8,128)S(1)} %broadcast_select_fusion.12), channel_id=1, source_target_pairs={{0,2},{1,3},{2,0},{3,1},{4,6},{5,7},{6,4},{7,5},{8,10},{9,11},{10,... | collective-permute-start | bytes 491528 | tf_op jit(solution)/shard_map/while/body/eval_jaxpr/ppermute | solution.py:17
  462.0 13.9 %collective-permute-start.7 = (bf16[64,2048]{1,0:T(8,128)(2,1)S(1)}, bf16[64,2048]{1,0:T(8,128)(2,1)S(1)}, u32[]{:S(2)}, u32[]{:S(2)}) collective-permute-start(bf16[64,2048]{1,0:T(8,128)(2,1)S(1)} %get-tuple-element.698), channel_id=1, source_target_pairs={{0,4},{1,5},{2,6},{3,7},{4,8},{5,9},{6,10},{7,11},{8,12},{9,13},{1... | collective-permute-start | bytes 786440 | tf_op jit(solution)/shard_map/while/body/eval_jaxpr/ppermute | solution.py:23
  464.8 5.9 %collective-permute-start.5 = (bf16[32,1024]{1,0:T(8,128)(2,1)S(1)}, bf16[32,1024]{1,0:T(8,128)(2,1)S(1)}, u32[]{:S(2)}, u32[]{:S(2)}) collective-permute-start(bf16[32,1024]{1,0:T(8,128)(2,1)S(1)} %maximum_select_fusion.2), channel_id=1, source_target_pairs={{0,2},{1,3},{2,0},{3,1},{4,6},{5,7},{6,4},{7,5},{8,10},{9,11},{10,... | collective-permute-start | bytes 196616 | tf_op jit(solution)/shard_map/while/body/eval_jaxpr/ppermute | solution.py:17
  470.7 21.1 %collective-permute-start.6 = (bf16[64,2048]{1,0:T(8,128)(2,1)S(1)}, bf16[64,2048]{1,0:T(8,128)(2,1)S(1)}, u32[]{:S(2)}, u32[]{:S(2)}) collective-permute-start(bf16[64,2048]{1,0:T(8,128)(2,1)S(1)} %get-tuple-element.798), channel_id=1, source_target_pairs={{0,4},{1,5},{2,6},{3,7},{4,8},{5,9},{6,10},{7,11},{8,12},{9,13},{1... | collective-permute-start | bytes 786440 | tf_op jit(solution)/shard_map/while/body/eval_jaxpr/ppermute | solution.py:23
  498.6 5.2 collective-permute-start.2
  502.1 6.9 %collective-permute-start = (f32[32,1280]{1,0:T(8,128)S(1)}, f32[32,1280]{1,0:T(8,128)S(1)}, u32[]{:S(2)}, u32[]{:S(2)}) collective-permute-start(f32[32,1280]{1,0:T(8,128)S(1)} %broadcast_select_fusion.12), channel_id=1, source_target_pairs={{0,2},{1,3},{2,0},{3,1},{4,6},{5,7},{6,4},{7,5},{8,10},{9,11},{10,... | collective-permute-start | bytes 491528 | tf_op jit(solution)/shard_map/while/body/eval_jaxpr/ppermute | solution.py:17
  513.7 4.7 collective-permute-start.4
  515.0 12.4 %collective-permute-start.7 = (bf16[64,2048]{1,0:T(8,128)(2,1)S(1)}, bf16[64,2048]{1,0:T(8,128)(2,1)S(1)}, u32[]{:S(2)}, u32[]{:S(2)}) collective-permute-start(bf16[64,2048]{1,0:T(8,128)(2,1)S(1)} %get-tuple-element.698), channel_id=1, source_target_pairs={{0,4},{1,5},{2,6},{3,7},{4,8},{5,9},{6,10},{7,11},{8,12},{9,13},{1... | collective-permute-start | bytes 786440 | tf_op jit(solution)/shard_map/while/body/eval_jaxpr/ppermute | solution.py:23
  518.5 5.9 %collective-permute-start.5 = (bf16[32,1024]{1,0:T(8,128)(2,1)S(1)}, bf16[32,1024]{1,0:T(8,128)(2,1)S(1)}, u32[]{:S(2)}, u32[]{:S(2)}) collective-permute-start(bf16[32,1024]{1,0:T(8,128)(2,1)S(1)} %maximum_select_fusion.2), channel_id=1, source_target_pairs={{0,2},{1,3},{2,0},{3,1},{4,6},{5,7},{6,4},{7,5},{8,10},{9,11},{10,... | collective-permute-start | bytes 196616 | tf_op jit(solution)/shard_map/while/body/eval_jaxpr/ppermute | solution.py:17
  524.4 14.4 %collective-permute-start.6 = (bf16[64,2048]{1,0:T(8,128)(2,1)S(1)}, bf16[64,2048]{1,0:T(8,128)(2,1)S(1)}, u32[]{:S(2)}, u32[]{:S(2)}) collective-permute-start(bf16[64,2048]{1,0:T(8,128)(2,1)S(1)} %get-tuple-element.798), channel_id=1, source_target_pairs={{0,4},{1,5},{2,6},{3,7},{4,8},{5,9},{6,10},{7,11},{8,12},{9,13},{1... | collective-permute-start | bytes 786440 | tf_op jit(solution)/shard_map/while/body/eval_jaxpr/ppermute | solution.py:23
  543.2 16.5 %collective-permute-start.8 = (bf16[512,1024]{0,1:T(8,128)(2,1)S(1)}, bf16[512,1024]{0,1:T(8,128)(2,1)}, u32[]{:S(2)}, u32[]{:S(2)}) collective-permute-start(bf16[512,1024]{0,1:T(8,128)(2,1)S(1)} %select_bitcast_fusion), channel_id=1, source_target_pairs={{0,8},{1,9},{2,10},{3,11},{4,12},{5,13},{6,14},{7,15},{8,0},{9,1},... | collective-permute-start | bytes 3145736 | tf_op jit(solution)/shard_map/ppermute | solution.py:17
  561.4 9.3 %collective-permute-start.9 = (bf16[512,512]{0,1:T(8,128)(2,1)S(1)}, bf16[512,512]{0,1:T(8,128)(2,1)S(1)}, u32[]{:S(2)}, u32[]{:S(2)}) collective-permute-start(bf16[512,512]{0,1:T(8,128)(2,1)S(1)} %select_bitcast_fusion.1), channel_id=1, source_target_pairs={{0,4},{1,5},{2,6},{3,7},{4,0},{5,1},{6,2},{7,3},{8,12},{9,13},{10,... | collective-permute-start | bytes 1572872 | tf_op jit(solution)/shard_map/ppermute | solution.py:17
  (28 other events, 111.2 us)
where the time goes:
time: 575 us; the launch traced here: 572 us
  waiting for transfers between devices  274 us (48%)
  starting transfers between devices  126 us (22%)
  matrix products  70.7 us (12%)
  loops' own time  48.5 us (8%)
  other arithmetic  31.8 us (6%)
  local copies, waits for them, and re-layouts  20.1 us (3%)
    ppermute x68, waiting for transfers between devices, partner(): lax.ppermute(value, axis, [(i, i ^ 1 << distance) for i in range(lax.axis...  180 us
    ppermute x68, starting transfers between devices, partner(): lax.ppermute(value, axis, [(i, i ^ 1 << distance) for i in range(lax.axis...  101 us
    ppermute x22, waiting for transfers between devices, shifted(): return lax.ppermute(value, axis, pairs)  94.2 us
    another operation x1, loops' own time, body(): lax.scan(advance, start, jnp.arange(MICRO + cycle_size - 1, dtype=jnp.int...  47.3 us
    dot_general x8, matrix products, local_partials(): jnp.dot(scaled, proj_weight, preferred_element_type=jnp.float32)  28 us
    ppermute x22, starting transfers between devices, shifted(): return lax.ppermute(value, axis, pairs)  25.2 us
    dot_general x8, matrix products, local_update(): jnp.dot(collected, out_weight, preferred_element_type=jnp.float32)  24.5 us
    select_n x11, other arithmetic, advance(): relayed = jnp.where(on_turn & (segment_index > 0), own_block, arriving)  11.9 us
  transfers between devices with their start and end apart: 90, of which 66 were waited for; matrix products, arithmetic and copies ran while one was open for 5% of the time, Pallas kernels for 0%

commit v1 on v0

v1 whole, which is shorter than its diff:
```python
import functools
import math

import jax
import jax.numpy as jnp
from jax import lax
from jax.experimental import pallas as pl
from jax.experimental.pallas import tpu as pltpu
from jax.sharding import PartitionSpec as P

BLOCK = 64
MICRO = 8
EPSILON = 1e-05
NEGATIVE = -1e30
TAIL = 128
MESH = pl.DeviceIdType.MESH
F32 = jnp.float32
BF16 = jnp.bfloat16


def kernel(
    shards,
    layers,
    hidden,
    gain,
    wq_hbm,
    wo_hbm,
    cache_hbm,
    exits,
    lens,
    out,
    wq,
    wo,
    cache,
    inb,
    outb,
    accs,
    rs_send,
    rs_recv,
    att,
    w_sem,
    hid_ss,
    in_rs,
    rs_ss,
    rs_rs,
    ag_ss,
    ag_rs,
    st_ss,
    out_rs,
):
    me = lax.axis_index("section")
    y = me // shards
    x = me % shards
    last = layers - 1
    span = inb.shape[3]
    group = BLOCK // shards
    query_width = wo.shape[1]
    width = wq.shape[2]
    head = (width - query_width) // 2
    heads = query_width // head
    context = cache.shape[0] // (MICRO * group)
    total_width = span * shards * layers

    def remote(src, dst, send_sem, recv_sem, target):
        return pltpu.make_async_remote_copy(
            src_ref=src,
            dst_ref=dst,
            send_sem=send_sem,
            recv_sem=recv_sem,
            device_id={"section": target},
            device_id_type=MESH,
        )

    def row_peer(d):
        return y * shards + (x + d) % shards

    wq_copies = [
        pltpu.make_async_copy(wq_hbm.at[pl.ds(j * span, span)], wq.at[j], w_sem.at[j])
        for j in range(layers)
    ]
    wo_copies = [
        pltpu.make_async_copy(
            wo_hbm.at[:, pl.ds(j * span, span)], wo.at[j], w_sem.at[layers + j]
        )
        for j in range(layers)
    ]
    cache_copy = pltpu.make_async_copy(cache_hbm, cache, w_sem.at[2 * layers])
    for copy in wq_copies:
        copy.start()
    cache_copy.start()
    for copy in wo_copies:
        copy.start()

    barrier = pltpu.get_barrier_semaphore()
    for d in range(1, shards):
        pl.semaphore_signal(
            barrier, inc=1, device_id={"section": row_peer(d)}, device_id_type=MESH
        )
    for d in range(1, layers):
        pl.semaphore_signal(
            barrier,
            inc=1,
            device_id={"section": ((y + d) % layers) * shards + x},
            device_id_type=MESH,
        )
    pl.semaphore_wait(barrier, shards + layers - 2)

    rounds = MICRO // layers
    place = (layers - y) % layers

    def hidden_piece(q, j):
        return hidden.at[pl.ds(q * BLOCK, BLOCK), pl.ds(j * span, span)]

    def hidden_copy(q, j):
        m = q * layers + place
        return remote(
            hidden_piece(q, j), inb.at[m, j], hid_ss.at[q, j], in_rs.at[m, j], x
        )

    @pl.when(y == 0)
    def _():
        for q in range(rounds):
            for j in range(layers):
                pltpu.make_async_copy(
                    hidden_piece(q, j), inb.at[q * layers, j], in_rs.at[q * layers, j]
                ).start()

    @pl.when(y != 0)
    def _():
        for q in range(rounds):
            for j in range(layers):
                hidden_copy(q, j).start()

    def rs_copy(i, d):
        target = (x + d) % shards
        return remote(
            rs_send.at[i, target],
            rs_recv.at[i, x],
            rs_ss.at[i, d - 1],
            rs_rs.at[i, x],
            row_peer(d),
        )

    def rs_arrival(i, d):
        source = (x + d) % shards
        return remote(
            rs_send.at[i, source],
            rs_recv.at[i, source],
            rs_ss.at[i, d - 1],
            rs_rs.at[i, source],
            row_peer(d),
        )

    def ag_copy(i, d):
        return remote(
            att.at[i, x], att.at[i, x], ag_ss.at[i, d - 1], ag_rs.at[i, x], row_peer(d)
        )

    def ag_arrival(i, d):
        source = (x + d) % shards
        return remote(
            att.at[i, source],
            att.at[i, source],
            ag_ss.at[i, d - 1],
            ag_rs.at[i, source],
            row_peer(d),
        )

    def state_copy(i, j):
        return remote(
            outb.at[i, j],
            inb.at[i, j],
            st_ss.at[i, j],
            in_rs.at[i, j],
            (me + shards) % (shards * layers),
        )

    def out_rows(i):
        return pl.ds(pl.multiple_of(i * BLOCK, BLOCK), BLOCK)

    def result_copy(i, j):
        return remote(
            outb.at[i, j], out.at[out_rows(i)], st_ss.at[i, j], out_rs.at[i], j * shards + x
        )

    def project(i):
        squares = jnp.zeros((BLOCK, TAIL), F32)
        acc = None
        for j in range(layers):

            @pl.when(i == 0)
            def _():
                wq_copies[j].wait()

            state_copy(i, j).wait_recv()
            state = inb[i, j].astype(F32)
            scaled = (state * gain[:, pl.ds(j * span, span)].astype(F32)).astype(BF16)
            squared = state * state
            for n in range(span // TAIL):
                squares = squares + squared[:, n * TAIL : (n + 1) * TAIL]
            part = jnp.dot(scaled, wq[j], preferred_element_type=F32)
            acc = part if acc is None else acc + part
        total = jnp.sum(squares, axis=1, keepdims=True)
        coarse = total.astype(BF16).astype(F32)
        lane = lax.broadcasted_iota(jnp.int32, (BLOCK, TAIL), 1)
        tail = jnp.where(lane < TAIL // 2, coarse, total - coarse)
        accs[:, :width] = acc
        accs[:, width:] = tail
        narrow = acc.astype(BF16)
        narrow_tail = tail.astype(BF16)
        for g in range(shards):
            rs_send[i, g, :, :width] = narrow[g * group : (g + 1) * group]
            rs_send[i, g, :, width:] = narrow_tail[g * group : (g + 1) * group]
        for d in (2, 1, 3):
            rs_copy(i, d).start()

    def attend(i):
        @pl.when(i == 0)
        def _():
            cache_copy.wait()

        summed = accs[pl.ds(pl.multiple_of(x * group, group), group), :]
        for d in (1, 3, 2):
            rs_arrival(i, d).wait_recv()
        for d in (1, 3, 2):
            summed = summed + rs_recv[i, (x + d) % shards].astype(F32)
        squares = jnp.sum(summed[:, width:], axis=1, keepdims=True) * (2.0 / TAIL)
        scale = lax.rsqrt(squares / total_width + EPSILON)
        fitted = summed[:, :width] * scale
        query = (fitted[:, :query_width] * (1.0 / math.sqrt(head))).astype(BF16)
        query = jnp.concatenate(
            [query[:, h * head : (h + 1) * head] for h in range(heads)], axis=0
        )
        key_new = fitted[:, query_width : query_width + head].astype(BF16).astype(F32)
        value_new = fitted[:, query_width + head :].astype(BF16).astype(F32)
        key_new = jnp.concatenate([key_new] * heads, axis=0)
        value_new = jnp.concatenate([value_new] * heads, axis=0)
        rows = pl.ds(pl.multiple_of(i * (group * context), group * context), group * context)
        keys = cache[rows, :head]
        values = cache[rows, head:]
        scores = lax.dot_general(
            query, keys, (((1,), (1,)), ((), ())), preferred_element_type=F32
        )
        own = jnp.sum(query.astype(F32) * key_new, axis=1, keepdims=True)
        span_of = lens[pl.ds(pl.multiple_of(i * BLOCK + x * group, group), group), :]
        span_of = jnp.concatenate([span_of] * (group * context // TAIL), axis=1)
        span_of = jnp.concatenate([span_of] * heads, axis=0)
        shape = (heads * group, group * context)
        row = lax.broadcasted_iota(jnp.int32, shape, 0)
        column = lax.broadcasted_iota(jnp.int32, shape, 1)
        offset = column - (row % group) * context
        usable = (offset >= 0) & (offset < span_of)
        scores = jnp.where(usable, scores, NEGATIVE)
        top = jnp.maximum(jnp.max(scores, axis=1, keepdims=True), own)
        raw = jnp.where(usable, jnp.exp(scores - top), 0.0)
        raw_own = jnp.exp(own - top)
        total = jnp.sum(raw, axis=1, keepdims=True) + raw_own
        inverse = 1.0 / total
        weights = (raw * inverse).astype(BF16)
        own_weight = (raw_own * inverse).astype(BF16).astype(F32)
        attended = jnp.dot(weights, values, preferred_element_type=F32)
        attended = (attended + own_weight * value_new).astype(BF16)
        att[i, x] = jnp.concatenate(
            [attended[h * group : (h + 1) * group] for h in range(heads)], axis=1
        )
        for d in (2, 1, 3):
            ag_copy(i, d).start()

    def update(i):
        for d in (1, 3, 2):
            ag_arrival(i, d).wait_recv()
        attended = att[i].reshape(BLOCK, query_width)
        depth = exits[out_rows(i), :]
        active = jnp.concatenate([depth] * (span // TAIL), axis=1) > y
        for j in range(layers):

            @pl.when(i == 0)
            def _():
                wo_copies[j].wait()

            state = inb[i, j].astype(F32)
            branch = jnp.dot(attended, wo[j], preferred_element_type=F32)
            updated = jnp.where(active, state + branch, state).astype(BF16)
            outb[i, j] = updated

            @pl.when(y < last)
            def _():
                state_copy(i, j).start()

            if j < last:

                @pl.when(y == last)
                def _():
                    result_copy(i, j).start()

            else:

                @pl.when(y == last)
                def _():
                    out[out_rows(i), :] = updated

    def step(i, carry):
        @pl.when(i < MICRO)
        def _():
            project(i)

        @pl.when(i > 0)
        def _():
            update(i - 1)

        @pl.when(i < MICRO)
        def _():
            attend(i)

        return carry

    lax.fori_loop(0, MICRO + 1, step, 0)

    def finish(i, carry):
        for d in range(1, shards):
            rs_copy(i, d).wait_send()
            ag_copy(i, d).wait_send()
        for j in range(layers):

            @pl.when(y < last)
            def _():
                state_copy(i, j).wait_send()

            if j < last:

                @pl.when(y == last)
                def _():
                    result_copy(i, j).wait_send()

        @pl.when(y < last)
        def _():
            result_copy(i, 0).wait_recv()

        return carry

    lax.fori_loop(0, MICRO, finish, 0)

    @pl.when(y != 0)
    def _():
        for q in range(rounds):
            for j in range(layers):
                hidden_copy(q, j).wait_send()


def body(hidden, exit_layer, lengths, kv_cache, norm_gain, w_qkv, w_out):
    devices = lax.axis_size("section")
    shards = max(2, devices // 4)
    layers = devices // shards
    own_hidden = hidden[0]
    proj_weight = w_qkv[0]
    out_weight = w_out[0]
    tokens = exit_layer.shape[0]
    quarter, width = proj_weight.shape
    query_width = out_weight.shape[0]
    span = quarter // layers
    group = BLOCK // shards
    cache_rows = kv_cache.shape[1] * kv_cache.shape[2]
    cache = kv_cache.reshape(cache_rows, kv_cache.shape[3])
    exits = jnp.broadcast_to(exit_layer[:, None], (tokens, TAIL))
    lens = jnp.broadcast_to(lengths[:, None], (tokens, TAIL))
    anywhere = pl.BlockSpec(memory_space=pl.ANY)
    vmem = pl.BlockSpec(memory_space=pltpu.VMEM)
    dma = pltpu.SemaphoreType.DMA
    return pl.pallas_call(
        functools.partial(kernel, shards, layers),
        out_shape=jax.ShapeDtypeStruct((tokens, span), BF16),
        in_specs=[anywhere, vmem, anywhere, anywhere, anywhere, vmem, vmem],
        out_specs=vmem,
        scratch_shapes=[
            pltpu.VMEM((layers, span, width), BF16),
            pltpu.VMEM((layers, query_width, span), BF16),
            pltpu.VMEM(cache.shape, BF16),
            pltpu.VMEM((MICRO, layers, BLOCK, span), BF16),
            pltpu.VMEM((MICRO, layers, BLOCK, span), BF16),
            pltpu.VMEM((BLOCK, width + TAIL), F32),
            pltpu.VMEM((MICRO, shards, group, width + TAIL), BF16),
            pltpu.VMEM((MICRO, shards, group, width + TAIL), BF16),
            pltpu.VMEM((MICRO, shards, group, query_width), BF16),
            dma((2 * layers + 1,)),
            dma((MICRO // layers, layers)),
            dma((MICRO, layers)),
            dma((MICRO, shards - 1)),
            dma((MICRO, shards)),
            dma((MICRO, shards - 1)),
            dma((MICRO, shards)),
            dma((MICRO, layers)),
            dma((MICRO,)),
        ],
        compiler_params=pltpu.CompilerParams(
            collective_id=0, has_side_effects=True, vmem_limit_bytes=56 << 20
        ),
    )(own_hidden, norm_gain, proj_weight, out_weight, cache, exits, lens)


def solution(mesh):
    return jax.shard_map(
        body,
        mesh=mesh,
        in_specs=(
            P("section", "blk", None),
            P("blk"),
            P("blk"),
            P("section", "blk", None, None),
            P("section", None),
            P("section", None, None),
            P("section", None, None),
        ),
        out_specs=P("blk", "section"),
        check_vma=False,
    )
```

time: 575 us -> 132 us (0.23)
  waiting for transfers between devices: 274 us -> 0 us
  Pallas kernels: 0 us -> 127 us
  starting transfers between devices: 126 us -> 0 us
  matrix products: 70.7 us -> 0 us
  loops' own time: 48.5 us -> 0 us
  other arithmetic: 31.8 us -> 0 us
  local copies, waits for them, and re-layouts: 20.1 us -> 4.9 us
    ppermute x90 -> x0, waiting for transfers between devices: 274 us -> none  [the longest x68 180 us: partner(): lax.ppermute(value, axis, [(i, i ^ 1 << distance) for i in range(lax.axis...]
    pallas_call x0 -> x1, Pallas kernels: none -> 127 us  [body(): pl.pallas_call(functools.partial(kernel, shards, layers), out_shape=jax.S...]
    ppermute x90 -> x0, starting transfers between devices: 126 us -> none  [the longest x68 101 us: partner(): lax.ppermute(value, axis, [(i, i ^ 1 << distance) for i in range(lax.axis...]
    dot_general x40 -> x0, matrix products: 70.7 us -> none  [the longest x8 28 us: local_partials(): jnp.dot(scaled, proj_weight, preferred_element_type=jnp.float32)]
    another operation x34 -> x0, loops' own time: 48.5 us -> none  [the longest x1 47.3 us: body(): lax.scan(advance, start, jnp.arange(MICRO + cycle_size - 1, dtype=jnp.int...]
    select_n x68 -> x0, other arithmetic: 13.5 us -> none  [the longest x11 11.9 us: advance(): relayed = jnp.where(on_turn & (segment_index > 0), own_block, arriving)]
    dynamic_slice x19 -> x0, local copies, waits for them, and re-layouts: 13.4 us -> none  [the longest x11 7.31 us: body(): lax.scan(advance, start, jnp.arange(MICRO + cycle_size - 1, dtype=jnp.int...]
    reduce_sum x27 -> x0, other arithmetic: 11.2 us -> none  [the longest x11 8.46 us: advance(): gate = in_range & (jnp.sum(active.astype(jnp.int32)) > 0)]
  transfers between devices with their start and end apart: 90 -> 0, of which waited for: 66 -> 0; matrix products, arithmetic and copies ran while one was open for 5% -> 0% of each run, Pallas kernels for 0% -> 0%
where the time goes in v1:
time: 132 us
  Pallas kernels  127 us (96%)
  local copies, waits for them, and re-layouts  4.9 us (4%)
    pallas_call x1, Pallas kernels, body(): pl.pallas_call(functools.partial(kernel, shards, layers), out_shape=jax.S...  127 us

profile of v1, /device:TPU:32, one launch (start us, length us, event | category | flops | bytes accessed | tf_op | source)
XLA Modules:
  0.0 131.5 jit_solution(7504793479724661938)
XLA Ops:
  0.0 1.5 %broadcast_in_dim.4.exits = s32[512,128]{1,0:T(8,128)} broadcast(s32[512]{0:T(512)} %param.8), dimensions={0} | broadcast | bytes 264192 | tf_op jit(solution)/shard_map/broadcast_in_dim | solution.py:364
  1.5 1.5 %broadcast_in_dim.5.lens = s32[512,128]{1,0:T(8,128)} broadcast(s32[512]{0:T(512)} %param.9), dimensions={0} | broadcast | bytes 264192 | tf_op jit(solution)/shard_map/broadcast_in_dim | solution.py:365
  3.0 126.6 %shard_map.73 = bf16[512,512]{1,0:T(8,128)(2,1)} custom-call(bf16[128,2048]{1,0:T(8,128)(2,1)} %bitcast.7, bf16[1,2048]{1,0:T(2,128)(2,1)} %gain.1, bf16[2048,1280]{1,0:T(8,128)(2,1)} %bitcast.4, bf16[1024,2048]{1,0:T(8,128)(2,1)} %bitcast.5, bf16[2048,256]{1,0:T(8,128)(2,1)} %bitcast.6, s32[512,128]{1,0:T(8,128)} %broadcast_in_dim.4.exits, ...), custom_call_target="tpu_custom_call" | custom-call | tf_op jit(solution)/shard_map/pallas_call | solution.py:369
  129.6 1.9 %copy.9 = bf16[512,512]{1,0:T(8,128)(2,1)} copy(bf16[512,512]{1,0:T(8,128)(2,1)} %shard_map.73) | data formatting | bytes 1048576

commit v2 on v1

--- a/solution.py
+++ b/solution.py
@@ -10,6 +10,10 @@
 
 BLOCK = 64
 MICRO = 8
+PARTS = 2
+CHUNKS = MICRO * PARTS
+LAG_A = 1
+LAG_U = 2
 EPSILON = 1e-05
 NEGATIVE = -1e30
 TAIL = 128
@@ -26,14 +30,16 @@
     wq_hbm,
     wo_hbm,
     cache_hbm,
-    exits,
-    lens,
+    exit_rows,
+    length_rows,
     out,
     wq,
     wo,
     cache,
     inb,
     outb,
+    exits,
+    lens,
     accs,
     rs_send,
     rs_recv,
@@ -52,13 +58,13 @@
     y = me // shards
     x = me % shards
     last = layers - 1
-    span = inb.shape[3]
-    group = BLOCK // shards
+    group, span = inb.shape[3:]
+    rows = shards * group
     query_width = wo.shape[1]
     width = wq.shape[2]
     head = (width - query_width) // 2
     heads = query_width // head
-    context = cache.shape[0] // (MICRO * group)
+    context = cache.shape[0] // (CHUNKS * group)
     total_width = span * shards * layers
 
     def remote(src, dst, send_sem, recv_sem, target):
@@ -108,28 +114,39 @@
     rounds = MICRO // layers
     place = (layers - y) % layers
 
-    def hidden_piece(q, j):
-        return hidden.at[pl.ds(q * BLOCK, BLOCK), pl.ds(j * span, span)]
-
-    def hidden_copy(q, j):
-        m = q * layers + place
-        return remote(
-            hidden_piece(q, j), inb.at[m, j], hid_ss.at[q, j], in_rs.at[m, j], x
+    pieces = [
+        (q, h, j) for q in range(rounds) for h in range(PARTS) for j in range(layers)
+    ]
+
+    def hidden_piece(q, h, j):
+        return hidden.at[q, :, h, :, pl.ds(j * span, span)]
+
+    def hidden_copy(q, h, j):
+        i = (q * layers + place) * PARTS + h
+        return remote(
+            hidden_piece(q, h, j), inb.at[i, j], hid_ss.at[q, h, j], in_rs.at[i, j], x
         )
 
     @pl.when(y == 0)
     def _():
-        for q in range(rounds):
-            for j in range(layers):
-                pltpu.make_async_copy(
-                    hidden_piece(q, j), inb.at[q * layers, j], in_rs.at[q * layers, j]
-                ).start()
+        for q, h, j in pieces:
+            i = q * layers * PARTS + h
+            pltpu.make_async_copy(
+                hidden_piece(q, h, j), inb.at[i, j], in_rs.at[i, j]
+            ).start()
 
     @pl.when(y != 0)
     def _():
-        for q in range(rounds):
-            for j in range(layers):
-                hidden_copy(q, j).start()
+        for q, h, j in pieces:
+            hidden_copy(q, h, j).start()
+
+    for r in range(exit_rows.shape[0]):
+        for source, target in ((exit_rows, exits), (length_rows, lens)):
+            spread = jnp.broadcast_to(source[r : r + 1, :], (TAIL, TAIL)).T
+            count = TAIL // BLOCK
+            target[r * count : (r + 1) * count] = spread.reshape(
+                (count,) + target.shape[1:]
+            )
 
     def rs_copy(i, d):
         target = (x + d) % shards
@@ -175,16 +192,16 @@
             (me + shards) % (shards * layers),
         )
 
-    def out_rows(i):
-        return pl.ds(pl.multiple_of(i * BLOCK, BLOCK), BLOCK)
+    def tokens(ref, i):
+        return ref.at[i // PARTS, :, i % PARTS]
 
     def result_copy(i, j):
         return remote(
-            outb.at[i, j], out.at[out_rows(i)], st_ss.at[i, j], out_rs.at[i], j * shards + x
+            outb.at[i, j], tokens(out, i), st_ss.at[i, j], out_rs.at[i], j * shards + x
         )
 
     def project(i):
-        squares = jnp.zeros((BLOCK, TAIL), F32)
+        squares = jnp.zeros((rows, TAIL), F32)
         acc = None
         for j in range(layers):
 
@@ -193,7 +210,7 @@
                 wq_copies[j].wait()
 
             state_copy(i, j).wait_recv()
-            state = inb[i, j].astype(F32)
+            state = inb[i, j].astype(F32).reshape(rows, span)
             scaled = (state * gain[:, pl.ds(j * span, span)].astype(F32)).astype(BF16)
             squared = state * state
             for n in range(span // TAIL):
@@ -202,15 +219,14 @@
             acc = part if acc is None else acc + part
         total = jnp.sum(squares, axis=1, keepdims=True)
         coarse = total.astype(BF16).astype(F32)
-        lane = lax.broadcasted_iota(jnp.int32, (BLOCK, TAIL), 1)
+        lane = lax.broadcasted_iota(jnp.int32, (rows, TAIL), 1)
         tail = jnp.where(lane < TAIL // 2, coarse, total - coarse)
-        accs[:, :width] = acc
-        accs[:, width:] = tail
-        narrow = acc.astype(BF16)
-        narrow_tail = tail.astype(BF16)
         for g in range(shards):
-            rs_send[i, g, :, :width] = narrow[g * group : (g + 1) * group]
-            rs_send[i, g, :, width:] = narrow_tail[g * group : (g + 1) * group]
+            part = slice(g * group, (g + 1) * group)
+            accs[i, g, :, :width] = acc[part]
+            accs[i, g, :, width:] = tail[part]
+            rs_send[i, g, :, :width] = acc[part].astype(BF16)
+            rs_send[i, g, :, width:] = tail[part].astype(BF16)
         for d in (2, 1, 3):
             rs_copy(i, d).start()
 
@@ -219,7 +235,7 @@
         def _():
             cache_copy.wait()
 
-        summed = accs[pl.ds(pl.multiple_of(x * group, group), group), :]
+        summed = accs[i, x]
         for d in (1, 3, 2):
             rs_arrival(i, d).wait_recv()
         for d in (1, 3, 2):
@@ -227,29 +243,29 @@
         squares = jnp.sum(summed[:, width:], axis=1, keepdims=True) * (2.0 / TAIL)
         scale = lax.rsqrt(squares / total_width + EPSILON)
         fitted = summed[:, :width] * scale
-        query = (fitted[:, :query_width] * (1.0 / math.sqrt(head))).astype(BF16)
+        query = fitted[:, :query_width] * (1.0 / math.sqrt(head))
         query = jnp.concatenate(
             [query[:, h * head : (h + 1) * head] for h in range(heads)], axis=0
-        )
+        ).astype(BF16)
         key_new = fitted[:, query_width : query_width + head].astype(BF16).astype(F32)
         value_new = fitted[:, query_width + head :].astype(BF16).astype(F32)
         key_new = jnp.concatenate([key_new] * heads, axis=0)
         value_new = jnp.concatenate([value_new] * heads, axis=0)
-        rows = pl.ds(pl.multiple_of(i * (group * context), group * context), group * context)
-        keys = cache[rows, :head]
-        values = cache[rows, head:]
+        held = group * context
+        keys = cache[pl.ds(pl.multiple_of(i * held, held), held), :head]
+        values = cache[pl.ds(pl.multiple_of(i * held, held), held), head:]
         scores = lax.dot_general(
             query, keys, (((1,), (1,)), ((), ())), preferred_element_type=F32
         )
         own = jnp.sum(query.astype(F32) * key_new, axis=1, keepdims=True)
-        span_of = lens[pl.ds(pl.multiple_of(i * BLOCK + x * group, group), group), :]
-        span_of = jnp.concatenate([span_of] * (group * context // TAIL), axis=1)
-        span_of = jnp.concatenate([span_of] * heads, axis=0)
-        shape = (heads * group, group * context)
+        reach = lens[i // PARTS, x, i % PARTS]
+        reach = jnp.concatenate([reach] * (held // TAIL), axis=1)
+        reach = jnp.concatenate([reach] * heads, axis=0)
+        shape = (heads * group, held)
         row = lax.broadcasted_iota(jnp.int32, shape, 0)
         column = lax.broadcasted_iota(jnp.int32, shape, 1)
         offset = column - (row % group) * context
-        usable = (offset >= 0) & (offset < span_of)
+        usable = (offset >= 0) & (offset < reach)
         scores = jnp.where(usable, scores, NEGATIVE)
         top = jnp.maximum(jnp.max(scores, axis=1, keepdims=True), own)
         raw = jnp.where(usable, jnp.exp(scores - top), 0.0)
@@ -259,18 +275,18 @@
         weights = (raw * inverse).astype(BF16)
         own_weight = (raw_own * inverse).astype(BF16).astype(F32)
         attended = jnp.dot(weights, values, preferred_element_type=F32)
-        attended = (attended + own_weight * value_new).astype(BF16)
+        attended = attended + own_weight * value_new
         att[i, x] = jnp.concatenate(
             [attended[h * group : (h + 1) * group] for h in range(heads)], axis=1
-        )
+        ).astype(BF16)
         for d in (2, 1, 3):
             ag_copy(i, d).start()
 
     def update(i):
         for d in (1, 3, 2):
             ag_arrival(i, d).wait_recv()
-        attended = att[i].reshape(BLOCK, query_width)
-        depth = exits[out_rows(i), :]
+        attended = att[i].astype(F32).reshape(rows, query_width).astype(BF16)
+        depth = exits[i // PARTS, :, i % PARTS].reshape(rows, TAIL)
         active = jnp.concatenate([depth] * (span // TAIL), axis=1) > y
         for j in range(layers):
 
@@ -278,9 +294,10 @@
             def _():
                 wo_copies[j].wait()
 
-            state = inb[i, j].astype(F32)
+            state = inb[i, j].astype(F32).reshape(rows, span)
             branch = jnp.dot(attended, wo[j], preferred_element_type=F32)
-            updated = jnp.where(active, state + branch, state).astype(BF16)
+            updated = jnp.where(active, state + branch, state)
+            updated = updated.reshape(shards, group, span).astype(BF16)
             outb[i, j] = updated
 
             @pl.when(y < last)
@@ -297,24 +314,24 @@
 
                 @pl.when(y == last)
                 def _():
-                    out[out_rows(i), :] = updated
+                    out[i // PARTS, :, i % PARTS] = updated
 
     def step(i, carry):
-        @pl.when(i < MICRO)
+        @pl.when(i < CHUNKS)
         def _():
             project(i)
 
-        @pl.when(i > 0)
+        @pl.when((i >= LAG_A) & (i < CHUNKS + LAG_A))
         def _():
-            update(i - 1)
-
-        @pl.when(i < MICRO)
+            attend(i - LAG_A)
+
+        @pl.when(i >= LAG_U)
         def _():
-            attend(i)
+            update(i - LAG_U)
 
         return carry
 
-    lax.fori_loop(0, MICRO + 1, step, 0)
+    lax.fori_loop(0, CHUNKS + LAG_U, step, 0)
 
     def finish(i, carry):
         for d in range(1, shards):
@@ -338,13 +355,12 @@
 
         return carry
 
-    lax.fori_loop(0, MICRO, finish, 0)
+    lax.fori_loop(0, CHUNKS, finish, 0)
 
     @pl.when(y != 0)
     def _():
-        for q in range(rounds):
-            for j in range(layers):
-                hidden_copy(q, j).wait_send()
+        for q, h, j in pieces:
+            hidden_copy(q, h, j).wait_send()
 
 
 def body(hidden, exit_layer, lengths, kv_cache, norm_gain, w_qkv, w_out):
@@ -358,43 +374,48 @@
     quarter, width = proj_weight.shape
     query_width = out_weight.shape[0]
     span = quarter // layers
-    group = BLOCK // shards
+    group = BLOCK // shards // PARTS
     cache_rows = kv_cache.shape[1] * kv_cache.shape[2]
     cache = kv_cache.reshape(cache_rows, kv_cache.shape[3])
-    exits = jnp.broadcast_to(exit_layer[:, None], (tokens, TAIL))
-    lens = jnp.broadcast_to(lengths[:, None], (tokens, TAIL))
+    exits = exit_layer.reshape(tokens // TAIL, TAIL)
+    lens = lengths.reshape(tokens // TAIL, TAIL)
+    own_hidden = own_hidden.reshape(MICRO // layers, shards, PARTS, group, quarter)
     anywhere = pl.BlockSpec(memory_space=pl.ANY)
     vmem = pl.BlockSpec(memory_space=pltpu.VMEM)
     dma = pltpu.SemaphoreType.DMA
-    return pl.pallas_call(
+    column = (MICRO, shards, PARTS, group, TAIL)
+    settled = pl.pallas_call(
         functools.partial(kernel, shards, layers),
-        out_shape=jax.ShapeDtypeStruct((tokens, span), BF16),
+        out_shape=jax.ShapeDtypeStruct((MICRO, shards, PARTS, group, span), BF16),
         in_specs=[anywhere, vmem, anywhere, anywhere, anywhere, vmem, vmem],
         out_specs=vmem,
         scratch_shapes=[
             pltpu.VMEM((layers, span, width), BF16),
             pltpu.VMEM((layers, query_width, span), BF16),
             pltpu.VMEM(cache.shape, BF16),
-            pltpu.VMEM((MICRO, layers, BLOCK, span), BF16),
-            pltpu.VMEM((MICRO, layers, BLOCK, span), BF16),
-            pltpu.VMEM((BLOCK, width + TAIL), F32),
-            pltpu.VMEM((MICRO, shards, group, width + TAIL), BF16),
-            pltpu.VMEM((MICRO, shards, group, width + TAIL), BF16),
-            pltpu.VMEM((MICRO, shards, group, query_width), BF16),
+            pltpu.VMEM((CHUNKS, layers, shards, group, span), BF16),
+            pltpu.VMEM((CHUNKS, layers, shards, group, span), BF16),
+            pltpu.VMEM(column, jnp.int32),
+            pltpu.VMEM(column, jnp.int32),
+            pltpu.VMEM((CHUNKS, shards, group, width + TAIL), F32),
+            pltpu.VMEM((CHUNKS, shards, group, width + TAIL), BF16),
+            pltpu.VMEM((CHUNKS, shards, group, width + TAIL), BF16),
+            pltpu.VMEM((CHUNKS, shards, group, query_width), BF16),
             dma((2 * layers + 1,)),
-            dma((MICRO // layers, layers)),
-            dma((MICRO, layers)),
-            dma((MICRO, shards - 1)),
-            dma((MICRO, shards)),
-            dma((MICRO, shards - 1)),
-            dma((MICRO, shards)),
-            dma((MICRO, layers)),
-            dma((MICRO,)),
+            dma((MICRO // layers, PARTS, layers)),
+            dma((CHUNKS, layers)),
+            dma((CHUNKS, shards - 1)),
+            dma((CHUNKS, shards)),
+            dma((CHUNKS, shards - 1)),
+            dma((CHUNKS, shards)),
+            dma((CHUNKS, layers)),
+            dma((CHUNKS,)),
         ],
         compiler_params=pltpu.CompilerParams(
             collective_id=0, has_side_effects=True, vmem_limit_bytes=56 << 20
         ),
     )(own_hidden, norm_gain, proj_weight, out_weight, cache, exits, lens)
+    return settled.reshape(tokens, span)
 
 
 def solution(mesh):

time: 132 us -> 125 us (0.947)
  Pallas kernels: 127 us -> 123 us
  local copies, waits for them, and re-layouts: 4.9 us -> 1.87 us
    pallas_call x1, Pallas kernels: 127 us -> 123 us  [body(): pl.pallas_call(functools.partial(kernel, shards, layers), out_shape=jax.S...]
    broadcast_in_dim x2 -> x0, local copies, waits for them, and re-layouts: 3.03 us -> none  [the longest x1 1.52 us: body(): exits = jnp.broadcast_to(exit_layer[:, None], (tokens, TAIL))]
where the time goes in v2:
time: 125 us
  Pallas kernels  123 us (98%)
  local copies, waits for them, and re-layouts  1.87 us (1%)
    pallas_call x1, Pallas kernels, body(): pl.pallas_call(functools.partial(kernel, shards, layers), out_shape=jax.S...  123 us

profile of v2, /device:TPU:32, one launch (start us, length us, event | category | flops | bytes accessed | tf_op | source)
XLA Modules:
  0.0 124.5 jit_solution(4953263818329660187)
XLA Ops:
  0.0 122.6 %shard_map.73 = bf16[8,4,2,8,512]{4,3,2,1,0:T(8,128)(2,1)} custom-call(bf16[2,4,2,8,2048]{4,3,2,1,0:T(8,128)(2,1)} %bitcast.11, bf16[1,2048]{1,0:T(2,128)(2,1)} %gain.1, bf16[2048,1280]{1,0:T(8,128)(2,1)} %bitcast.7, bf16[1024,2048]{1,0:T(8,128)(2,1)} %bitcast.8, bf16[2048,256]{1,0:T(8,128)(2,1)} %bitcast.10, s32[4,128]{1,0:T(4,128)} %bitcast.12, ...), custom_call_target="tpu_custom_call" | custom-call | tf_op jit(solution)/shard_map/pallas_call | solution.py:387
  122.7 1.9 %copy.9 = bf16[512,512]{1,0:T(8,128)(2,1)} copy(bf16[512,512]{1,0:T(8,128)(2,1)} %bitcast.9) | data formatting | bytes 1048576

commit v3 on v2

--- a/solution.py
+++ b/solution.py
@@ -12,6 +12,13 @@
 MICRO = 8
 PARTS = 2
 CHUNKS = MICRO * PARTS
+CONTEXT = 16
+SORTED = 4
+KEEP = 16
+MAIN = 8
+DEEP = MAIN + 1
+TOTAL = DEEP + MAIN
+POSITION = ((0, 1, 9, 10), (2, 4, 11, 13), (6, 7, 15, 16), (3, 5, 12, 14))
 LAG_A = 1
 LAG_U = 2
 EPSILON = 1e-05
@@ -22,7 +29,7 @@
 BF16 = jnp.bfloat16
 
 
-def kernel(
+def full_kernel(
     shards,
     layers,
     hidden,
@@ -363,29 +370,549 @@
             hidden_copy(q, h, j).wait_send()
 
 
-def body(hidden, exit_layer, lengths, kv_cache, norm_gain, w_qkv, w_out):
-    devices = lax.axis_size("section")
-    shards = max(2, devices // 4)
-    layers = devices // shards
-    own_hidden = hidden[0]
-    proj_weight = w_qkv[0]
-    out_weight = w_out[0]
-    tokens = exit_layer.shape[0]
+def early_kernel(
+    shards,
+    layers,
+    hidden,
+    gain,
+    wq_hbm,
+    wo_hbm,
+    cache_hbm,
+    exit_rows,
+    length_rows,
+    out,
+    wq,
+    wo,
+    cache,
+    inb,
+    outb,
+    hid,
+    staged,
+    own_pick,
+    late_pick,
+    target,
+    settled,
+    exits,
+    lens,
+    starts,
+    accs,
+    rs_send,
+    rs_recv,
+    att,
+    w_sem,
+    hid_in,
+    hid_ss,
+    turn,
+    in_rs,
+    rs_ss,
+    rs_rs,
+    ag_ss,
+    ag_rs,
+    st_ss,
+    out_rs,
+):
+    me = lax.axis_index("section")
+    y = me // shards
+    x = me % shards
+    last = layers - 1
+    group, span = inb.shape[3:]
+    rows = shards * group
+    query_width = wo.shape[1]
+    width = wq.shape[2]
+    head = (width - query_width) // 2
+    heads = query_width // head
+    context = CONTEXT
+    count = DEEP + MAIN * ((last - y) // last)
+    total_width = span * shards * layers
+
+    def remote(src, dst, send_sem, recv_sem, target):
+        return pltpu.make_async_remote_copy(
+            src_ref=src,
+            dst_ref=dst,
+            send_sem=send_sem,
+            recv_sem=recv_sem,
+            device_id={"section": target},
+            device_id_type=MESH,
+        )
+
+    def row_peer(d):
+        return y * shards + (x + d) % shards
+
+    wq_copies = [
+        pltpu.make_async_copy(wq_hbm.at[pl.ds(j * span, span)], wq.at[j], w_sem.at[j])
+        for j in range(layers)
+    ]
+    wo_copies = [
+        pltpu.make_async_copy(
+            wo_hbm.at[:, pl.ds(j * span, span)], wo.at[j], w_sem.at[layers + j]
+        )
+        for j in range(layers)
+    ]
+    cache_copy = pltpu.make_async_copy(cache_hbm, cache, w_sem.at[2 * layers])
+    hid_copy = pltpu.make_async_copy(hidden, hid, hid_in.at[0])
+    hid_copy.start()
+    for copy in wq_copies:
+        copy.start()
+    cache_copy.start()
+    for copy in wo_copies:
+        copy.start()
+
+    barrier = pltpu.get_barrier_semaphore()
+    for d in range(1, shards):
+        pl.semaphore_signal(
+            barrier, inc=1, device_id={"section": row_peer(d)}, device_id_type=MESH
+        )
+    for d in range(1, layers):
+        pl.semaphore_signal(
+            barrier,
+            inc=1,
+            device_id={"section": ((y + d) % layers) * shards + x},
+            device_id_type=MESH,
+        )
+
+    wide = (TAIL, TAIL)
+    t0 = lax.broadcasted_iota(jnp.int32, wide, 0)
+    t1 = lax.broadcasted_iota(jnp.int32, wide, 1)
+    g0 = (t0 & (BLOCK - 1)) >> 4
+    g1 = (t1 & (BLOCK - 1)) >> 4
+    same = g0 == g1
+    lane_group = (t1 & 31) >> 3
+    lane_rank = ((t1 >> 5) << 3) + (t1 & 7)
+    slot_row = lax.broadcasted_iota(jnp.int32, (rows, TAIL), 0)
+    low_half = t1 < BLOCK
+    base_lane = jnp.zeros((1, TAIL), jnp.int32)
+    base_column = jnp.zeros((TAIL, 1), jnp.int32)
+    late = jnp.zeros((rows, 3 * TAIL), F32)
+
+    def piece_row(ref, p):
+        first = jnp.broadcast_to(ref[p // 2 : p // 2 + 1, :], wide)
+        second = jnp.broadcast_to(ref[p // 2 + 2 : p // 2 + 3, :], wide)
+        if p % 2 == 0:
+            return jnp.where(low_half, first, pltpu.roll(second, BLOCK, 1))
+        return jnp.where(low_half, pltpu.roll(first, BLOCK, 1), second)
+
+    def number(mask):
+        return jnp.where(mask, 1.0, 0.0)
+
+    for p in range(layers):
+        exit_row = piece_row(exit_rows, p)
+        exit_column = exit_row.T
+        length_column = piece_row(length_rows, p).T
+        ahead = same & (
+            (exit_column > exit_row) | ((exit_column == exit_row) & (t0 < t1))
+        )
+        rank_lane = jnp.sum(number(ahead), axis=0, keepdims=True).astype(jnp.int32)
+        behind = same & (
+            (exit_row > exit_column) | ((exit_row == exit_column) & (t1 < t0))
+        )
+        rank_column = jnp.sum(number(behind), axis=1, keepdims=True).astype(jnp.int32)
+        deep_column = jnp.sum(
+            number(same & (exit_row > 1)), axis=1, keepdims=True
+        ).astype(jnp.int32)
+        deep_lane = jnp.sum(
+            number((exit_column > 1) & (g0 == lane_group)), axis=0, keepdims=True
+        ).astype(jnp.int32)
+        order_lane = ((rank_lane >> 3) << 5) + (g1 << 3) + (rank_lane & 7)
+        order_column = ((rank_column >> 3) << 5) + (g0 << 3) + (rank_column & 7)
+        pick = number(order_lane == t0).astype(BF16)
+
+        @pl.when(y == (layers - p) % layers)
+        def _():
+            own_pick[...] = pick
+
+        natural = ((p + layers * (t0 >> 6)) << 4) + (t0 & 15)
+        facts = jnp.concatenate([exit_column, length_column, natural], axis=1)
+        sorted_facts = jnp.dot(
+            pick, facts.astype(F32).astype(BF16), preferred_element_type=F32
+        )
+        for c in range(SORTED):
+            block = sorted_facts[c * rows : (c + 1) * rows].astype(jnp.int32)
+            block = block.reshape(shards, group, 3 * TAIL)
+            exits[POSITION[p][c]] = block[:, :, :TAIL]
+            lens[POSITION[p][c]] = block[:, :, TAIL : 2 * TAIL]
+            starts[POSITION[p][c]] = block[:, :, 2 * TAIL :] * context
+        chosen = (
+            (lane_rank[:rows] >= KEEP)
+            & (lane_rank[:rows] < deep_lane)
+            & (lane_group[:rows] == (slot_row >> 3))
+            & (base_lane + lane_rank[:rows] - KEEP == (slot_row & 7))
+        )
+        chosen = number(chosen).astype(BF16)
+        late_pick[p] = chosen
+        late = late + jnp.dot(
+            chosen, sorted_facts.astype(BF16), preferred_element_type=F32
+        )
+        moved = (rank_column >= KEEP) & (rank_column < deep_column)
+        target[p] = jnp.where(
+            moved,
+            TAIL + (g0 << 3) + base_column + rank_column - KEEP,
+            order_column,
+        )
+        base_lane = base_lane + jnp.maximum(deep_lane - KEEP, 0)
+        base_column = base_column + jnp.maximum(deep_column - KEEP, 0)
+    late = late.astype(jnp.int32).reshape(shards, group, 3 * TAIL)
+    exits[MAIN] = late[:, :, :TAIL]
+    lens[MAIN] = late[:, :, TAIL : 2 * TAIL]
+    starts[MAIN] = late[:, :, 2 * TAIL :] * context
+
+    hid_copy.wait()
+    for j in range(layers):
+        ordered = jnp.dot(
+            own_pick[...],
+            hid[:, j * span : (j + 1) * span],
+            preferred_element_type=F32,
+        )
+        ordered = ordered.reshape(SORTED, shards, group, span).astype(BF16)
+
+        @pl.when(y == 0)
+        def _():
+            for c in range(SORTED):
+                inb[POSITION[0][c], j] = ordered[c]
+
+        @pl.when(y != 0)
+        def _():
+            for c in range(SORTED):
+                staged[c, j] = ordered[c]
+
+    pl.semaphore_wait(barrier, shards + layers - 2)
+
+    def hidden_copy(p, c, j):
+        i = POSITION[p][c]
+        return remote(
+            staged.at[c, j], inb.at[i, j], hid_ss.at[c, j], in_rs.at[i, j], x
+        )
+
+    def hidden_start(p, chunks):
+        for c in chunks:
+            for j in range(layers):
+                hidden_copy(p, c, j).start()
+
+    def hidden_sent(p, chunks):
+        for c in chunks:
+            for j in range(layers):
+                hidden_copy(p, c, j).wait_send()
+
+    for p in (1, 3):
+
+        @pl.when(y == layers - p)
+        def _():
+            hidden_start(p, (0, 1))
+            hidden_sent(p, (0, 1))
+            pl.semaphore_signal(
+                turn, inc=1, device_id={"section": 2 * shards + x}, device_id_type=MESH
+            )
+            hidden_start(p, (2, 3))
+
+    @pl.when(y == 2)
+    def _():
+        pl.semaphore_wait(turn, 2)
+        hidden_start(2, (0, 1, 2, 3))
+
+    def rs_copy(i, d):
+        target = (x + d) % shards
+        return remote(
+            rs_send.at[i, target],
+            rs_recv.at[i, x],
+            rs_ss.at[i, d - 1],
+            rs_rs.at[i, x],
+            row_peer(d),
+        )
+
+    def rs_arrival(i, d):
+        source = (x + d) % shards
+        return remote(
+            rs_send.at[i, source],
+            rs_recv.at[i, source],
+            rs_ss.at[i, d - 1],
+            rs_rs.at[i, source],
+            row_peer(d),
+        )
+
+    def ag_copy(i, d):
+        return remote(
+            att.at[i, x], att.at[i, x], ag_ss.at[i, d - 1], ag_rs.at[i, x], row_peer(d)
+        )
+
+    def ag_arrival(i, d):
+        source = (x + d) % shards
+        return remote(
+            att.at[i, source],
+            att.at[i, source],
+            ag_ss.at[i, d - 1],
+            ag_rs.at[i, source],
+            row_peer(d),
+        )
+
+    def state_copy(i, j):
+        return remote(
+            outb.at[i, j],
+            inb.at[i, j],
+            st_ss.at[i, j],
+            in_rs.at[i, j],
+            (me + shards) % (shards * layers),
+        )
+
+    def result_copy(i, j):
+        return remote(
+            outb.at[i, j], settled.at[i], st_ss.at[i, j], out_rs.at[i], j * shards + x
+        )
+
+    def gather_late():
+        for c in range(2, SORTED):
+            for p in range(1, layers):
+                for j in range(layers):
+                    state_copy(POSITION[p][c], j).wait_recv()
+        for j in range(layers):
+            found = None
+            for p in range(layers):
+                held = [inb[POSITION[p][c], j].astype(F32) for c in range(2, SORTED)]
+                held = [jnp.zeros_like(part) for part in held] + held
+                held = jnp.concatenate([part.reshape(rows, span) for part in held], axis=0)
+                part = jnp.dot(
+                    late_pick[p], held.astype(BF16), preferred_element_type=F32
+                )
+                found = part if found is None else found + part
+            inb[MAIN, j] = found.reshape(shards, group, span).astype(BF16)
+
+    def project(i):
+        squares = jnp.zeros((rows, TAIL), F32)
+        acc = None
+        for j in range(layers):
+
+            @pl.when(i == 0)
+            def _():
+                wq_copies[j].wait()
+
+            @pl.when((y > 0) | ((i > 1) & (i < MAIN)))
+            def _():
+                state_copy(i, j).wait_recv()
+
+            state = inb[i, j].astype(F32).reshape(rows, span)
+            scaled = (state * gain[:, pl.ds(j * span, span)].astype(F32)).astype(BF16)
+            squared = state * state
+            for n in range(span // TAIL):
+                squares = squares + squared[:, n * TAIL : (n + 1) * TAIL]
+            part = jnp.dot(scaled, wq[j], preferred_element_type=F32)
+            acc = part if acc is None else acc + part
+        total = jnp.sum(squares, axis=1, keepdims=True)
+        coarse = total.astype(BF16).astype(F32)
+        lane = lax.broadcasted_iota(jnp.int32, (rows, TAIL), 1)
+        tail = jnp.where(lane < TAIL // 2, coarse, total - coarse)
+        for g in range(shards):
+            part = slice(g * group, (g + 1) * group)
+            accs[i, g, :, :width] = acc[part]
+            accs[i, g, :, width:] = tail[part]
+            rs_send[i, g, :, :width] = acc[part].astype(BF16)
+            rs_send[i, g, :, width:] = tail[part].astype(BF16)
+        for d in (2, 1, 3):
+            rs_copy(i, d).start()
+
+    def attend(i):
+        @pl.when(i == 0)
+        def _():
+            cache_copy.wait()
+
+        b = i - DEEP * (i // DEEP)
+        p = ((b + 6) // 8) * (1 - b // 6) * (1 + 2 * (b % 2)) + 2 * (b // 6)
+        half = shards * shards * context
+
+        @pl.when(i == MAIN)
+        def _():
+            attend_over(i, [(0, cache.shape[0])])
+
+        @pl.when(i != MAIN)
+        def _():
+            attend_over(
+                i,
+                [
+                    (pl.multiple_of(p * half, half), half),
+                    (pl.multiple_of((p + layers) * half, half), half),
+                ],
+            )
+
+    def attend_over(i, pieces):
+
+        summed = accs[i, x]
+        for d in (1, 3, 2):
+            rs_arrival(i, d).wait_recv()
+        for d in (1, 3, 2):
+            summed = summed + rs_recv[i, (x + d) % shards].astype(F32)
+        squares = jnp.sum(summed[:, width:], axis=1, keepdims=True) * (2.0 / TAIL)
+        scale = lax.rsqrt(squares / total_width + EPSILON)
+        fitted = summed[:, :width] * scale
+        query = fitted[:, :query_width] * (1.0 / math.sqrt(head))
+        query = jnp.concatenate(
+            [query[:, h * head : (h + 1) * head] for h in range(heads)], axis=0
+        ).astype(BF16)
+        key_new = fitted[:, query_width : query_width + head].astype(BF16).astype(F32)
+        value_new = fitted[:, query_width + head :].astype(BF16).astype(F32)
+        key_new = jnp.concatenate([key_new] * heads, axis=0)
+        value_new = jnp.concatenate([value_new] * heads, axis=0)
+        keys = jnp.concatenate(
+            [cache[pl.ds(at, size), :head] for at, size in pieces], axis=0
+        )
+        values = jnp.concatenate(
+            [cache[pl.ds(at, size), head:] for at, size in pieces], axis=0
+        )
+        scores = lax.dot_general(
+            query, keys, (((1,), (1,)), ((), ())), preferred_element_type=F32
+        )
+        own = jnp.sum(query.astype(F32) * key_new, axis=1, keepdims=True)
+        def per_query(fact):
+            return jnp.concatenate([fact[i, x]] * heads, axis=0)
+
+        reach = per_query(lens)
+        start = per_query(starts)
+        offset = []
+        for at, size in pieces:
+            for n in range(size // TAIL):
+                lane = lax.broadcasted_iota(jnp.int32, start.shape, 1)
+                offset.append(lane + (at + n * TAIL) - start)
+        reach = jnp.concatenate([reach] * len(offset), axis=1)
+        offset = jnp.concatenate(offset, axis=1)
+        usable = (offset >= 0) & (offset < reach)
+        scores = jnp.where(usable, scores, NEGATIVE)
+        top = jnp.maximum(jnp.max(scores, axis=1, keepdims=True), own)
+        raw = jnp.where(usable, jnp.exp(scores - top), 0.0)
+        raw_own = jnp.exp(own - top)
+        total = jnp.sum(raw, axis=1, keepdims=True) + raw_own
+        inverse = 1.0 / total
+        weights = (raw * inverse).astype(BF16)
+        own_weight = (raw_own * inverse).astype(BF16).astype(F32)
+        attended = jnp.dot(weights, values, preferred_element_type=F32)
+        attended = attended + own_weight * value_new
+        att[i, x] = jnp.concatenate(
+            [attended[h * group : (h + 1) * group] for h in range(heads)], axis=1
+        ).astype(BF16)
+        for d in (2, 1, 3):
+            ag_copy(i, d).start()
+
+    def update(i):
+        for d in (1, 3, 2):
+            ag_arrival(i, d).wait_recv()
+        attended = att[i].astype(F32).reshape(rows, query_width).astype(BF16)
+        depth = exits[i].reshape(rows, TAIL)
+        final = ((y == last) & (i < DEEP)) | (i >= DEEP)
+        active = jnp.concatenate([depth] * (span // TAIL), axis=1) > y
+        for j in range(layers):
+
+            @pl.when(i == 0)
+            def _():
+                wo_copies[j].wait()
+
+            state = inb[i, j].astype(F32).reshape(rows, span)
+            branch = jnp.dot(attended, wo[j], preferred_element_type=F32)
+            updated = jnp.where(active, state + branch, state)
+            updated = updated.reshape(shards, group, span).astype(BF16)
+            outb[i, j] = updated
+
+            @pl.when((y < last) & (i < DEEP))
+            def _():
+                state_copy(i, j).start()
+
+            @pl.when(final & (y != j))
+            def _():
+                result_copy(i, j).start()
+
+            @pl.when(final & (y == j))
+            def _():
+                settled[i] = updated
+
+    def step(i, carry):
+        @pl.when((y == 0) & (i == MAIN))
+        def _():
+            gather_late()
+
+        @pl.when(i < count)
+        def _():
+            project(i)
+
+        @pl.when((i >= LAG_A) & (i < count + LAG_A))
+        def _():
+            attend(i - LAG_A)
+
+        @pl.when(i >= LAG_U)
+        def _():
+            update(i - LAG_U)
+
+        return carry
+
+    lax.fori_loop(0, count + LAG_U, step, 0)
+
+    def arrive(i, carry):
+        @pl.when(((y != last) & (i < DEEP)) | ((y != 0) & (i >= DEEP)))
+        def _():
+            result_copy(i, 0).wait_recv()
+
+        return carry
+
+    lax.fori_loop(0, TOTAL, arrive, 0)
+
+    reach = lax.broadcasted_iota(jnp.int32, wide, 1)
+    extra = settled[MAIN].astype(F32).reshape(rows, span)
+    extra = jnp.concatenate([extra] + [jnp.zeros_like(extra)] * (SORTED - 1), axis=0)
+    extra = extra.astype(BF16)
+    for p in range(layers):
+        found = jnp.concatenate(
+            [
+                settled[POSITION[p][c]].astype(F32).reshape(rows, span)
+                for c in range(SORTED)
+            ],
+            axis=0,
+        ).astype(BF16)
+        goal = target[p]
+        result = jnp.dot(
+            number(goal == reach).astype(BF16), found, preferred_element_type=F32
+        ) + jnp.dot(
+            number(goal == reach + TAIL).astype(BF16), extra, preferred_element_type=F32
+        )
+        result = result.astype(BF16)
+        out[p * BLOCK : (p + 1) * BLOCK, :] = result[:BLOCK]
+        out[(p + layers) * BLOCK : (p + layers + 1) * BLOCK, :] = result[BLOCK:]
+
+    def finish(i, carry):
+        for d in range(1, shards):
+            rs_copy(i, d).wait_send()
+            ag_copy(i, d).wait_send()
+        final = ((y == last) & (i < DEEP)) | (i >= DEEP)
+        for j in range(layers):
+
+            @pl.when((y < last) & (i < DEEP))
+            def _():
+                state_copy(i, j).wait_send()
+
+            @pl.when(final & (y != j))
+            def _():
+                result_copy(i, j).wait_send()
+
+        return carry
+
+    lax.fori_loop(0, count, finish, 0)
+
+    for p in (1, 3):
+
+        @pl.when(y == layers - p)
+        def _():
+            hidden_sent(p, (2, 3))
+
+    @pl.when(y == 2)
+    def _():
+        hidden_sent(2, (0, 1, 2, 3))
+
+
+def full(shards, layers, hidden, gain, proj_weight, out_weight, cache, exits, lens):
+    tokens = exits.shape[0] * exits.shape[1]
     quarter, width = proj_weight.shape
     query_width = out_weight.shape[0]
     span = quarter // layers
     group = BLOCK // shards // PARTS
-    cache_rows = kv_cache.shape[1] * kv_cache.shape[2]
-    cache = kv_cache.reshape(cache_rows, kv_cache.shape[3])
-    exits = exit_layer.reshape(tokens // TAIL, TAIL)
-    lens = lengths.reshape(tokens // TAIL, TAIL)
-    own_hidden = own_hidden.reshape(MICRO // layers, shards, PARTS, group, quarter)
+    hidden = hidden.reshape(MICRO // layers, shards, PARTS, group, quarter)
     anywhere = pl.BlockSpec(memory_space=pl.ANY)
     vmem = pl.BlockSpec(memory_space=pltpu.VMEM)
     dma = pltpu.SemaphoreType.DMA
     column = (MICRO, shards, PARTS, group, TAIL)
     settled = pl.pallas_call(
-        functools.partial(kernel, shards, layers),
+        functools.partial(full_kernel, shards, layers),
         out_shape=jax.ShapeDtypeStruct((MICRO, shards, PARTS, group, span), BF16),
         in_specs=[anywhere, vmem, anywhere, anywhere, anywhere, vmem, vmem],
         out_specs=vmem,
@@ -414,8 +941,82 @@
         compiler_params=pltpu.CompilerParams(
             collective_id=0, has_side_effects=True, vmem_limit_bytes=56 << 20
         ),
-    )(own_hidden, norm_gain, proj_weight, out_weight, cache, exits, lens)
+    )(hidden, gain, proj_weight, out_weight, cache, exits, lens)
     return settled.reshape(tokens, span)
+
+
+def early(shards, layers, hidden, gain, proj_weight, out_weight, cache, exits, lens):
+    tokens = exits.shape[0] * exits.shape[1]
+    quarter, width = proj_weight.shape
+    query_width = out_weight.shape[0]
+    span = quarter // layers
+    group = BLOCK // shards // PARTS
+    rows = shards * group
+    anywhere = pl.BlockSpec(memory_space=pl.ANY)
+    vmem = pl.BlockSpec(memory_space=pltpu.VMEM)
+    dma = pltpu.SemaphoreType.DMA
+    fact = (TOTAL, shards, group, TAIL)
+    return pl.pallas_call(
+        functools.partial(early_kernel, shards, layers),
+        out_shape=jax.ShapeDtypeStruct((tokens, span), BF16),
+        in_specs=[anywhere, vmem, anywhere, anywhere, anywhere, vmem, vmem],
+        out_specs=vmem,
+        scratch_shapes=[
+            pltpu.VMEM((layers, span, width), BF16),
+            pltpu.VMEM((layers, query_width, span), BF16),
+            pltpu.VMEM(cache.shape, BF16),
+            pltpu.VMEM((TOTAL, layers, shards, group, span), BF16),
+            pltpu.VMEM((TOTAL, layers, shards, group, span), BF16),
+            pltpu.VMEM(hidden.shape, BF16),
+            pltpu.VMEM((SORTED, layers, shards, group, span), BF16),
+            pltpu.VMEM((TAIL, TAIL), BF16),
+            pltpu.VMEM((layers, rows, TAIL), BF16),
+            pltpu.VMEM((layers, TAIL, TAIL), jnp.int32),
+            pltpu.VMEM((TOTAL, shards, group, span), BF16),
+            pltpu.VMEM(fact, jnp.int32),
+            pltpu.VMEM(fact, jnp.int32),
+            pltpu.VMEM(fact, jnp.int32),
+            pltpu.VMEM((TOTAL, shards, group, width + TAIL), F32),
+            pltpu.VMEM((TOTAL, shards, group, width + TAIL), BF16),
+            pltpu.VMEM((TOTAL, shards, group, width + TAIL), BF16),
+            pltpu.VMEM((TOTAL, shards, group, query_width), BF16),
+            dma((2 * layers + 1,)),
+            dma((1,)),
+            dma((SORTED, layers)),
+            pltpu.SemaphoreType.REGULAR,
+            dma((TOTAL, layers)),
+            dma((TOTAL, shards - 1)),
+            dma((TOTAL, shards)),
+            dma((TOTAL, shards - 1)),
+            dma((TOTAL, shards)),
+            dma((TOTAL, layers)),
+            dma((TOTAL,)),
+        ],
+        compiler_params=pltpu.CompilerParams(
+            collective_id=1, has_side_effects=True, vmem_limit_bytes=56 << 20
+        ),
+    )(hidden, gain, proj_weight, out_weight, cache, exits, lens)
+
+
+def body(hidden, exit_layer, lengths, kv_cache, norm_gain, w_qkv, w_out):
+    devices = lax.axis_size("section")
+    shards = max(2, devices // 4)
+    layers = devices // shards
+    tokens = exit_layer.shape[0]
+    cache = kv_cache.reshape(kv_cache.shape[1] * kv_cache.shape[2], kv_cache.shape[3])
+    exits = exit_layer.reshape(tokens // TAIL, TAIL)
+    lens = lengths.reshape(tokens // TAIL, TAIL)
+    operands = (hidden[0], norm_gain, w_qkv[0], w_out[0], cache, exits, lens)
+    going = (exit_layer > 1).astype(jnp.int32)
+    going = going.reshape(MICRO // layers, layers, shards, BLOCK // shards)
+    over = jnp.maximum(jnp.sum(going, axis=(0, 3)) - KEEP, 0)
+    fits = jnp.max(jnp.sum(over, axis=0)) <= BLOCK // shards // PARTS
+    return lax.cond(
+        fits,
+        functools.partial(early, shards, layers),
+        functools.partial(full, shards, layers),
+        *operands,
+    )
 
 
 def solution(mesh):

time: 125 us -> 97 us (0.78)
  Pallas kernels: 123 us -> 93.6 us
  other arithmetic: 0 us -> 1.5 us
    pallas_call x1, Pallas kernels: 123 us -> 93.6 us  [early(): pl.pallas_call(functools.partial(early_kernel, shards, layers), out_shape...]
where the time goes in v3:
time: 97 us; the launch traced here: 96.6 us
  Pallas kernels  93.6 us (96%)
  other arithmetic  1.5 us (2%)
    pallas_call x1, Pallas kernels, early(): pl.pallas_call(functools.partial(early_kernel, shards, layers), out_shape...  93.6 us

profile of v3, /device:TPU:32, one launch (start us, length us, event | category | flops | bytes accessed | tf_op | source)
XLA Modules:
  0.0 96.6 jit_solution(5567716266861347392)
XLA Ops:
  0.0 0.7 compare_convert_fusion
  0.7 0.1 reshape.30
  0.8 0.2 reduce_sum.18
  0.9 0.6 reduce_max.9
  2.2 93.6 %conditional.1 = (bf16[512,512]{1,0:T(8,128)(2,1)S(1)}) conditional(s32[]{:T(128)} %convert_element_type.4, (bf16[1,128,2048]{2,1,0:T(8,128)(2,1)}, bf16[1,2048]{1,0:T(2,128)(2,1)}, bf16[1,2048,1280]{2,1,0:T(8,128)(2,1)}, bf16[1,1024,2048]{2,1,0:T(8,128)(2,1)}, bf16[1,128,16,256]{3,2,1,0:T(8,128)(2,1)}, /*index=5*/s32[512]{0:T(512)}, ...), branch_computations={%region_3.0_spmd, %region_4.0_spmd} | conditional | bytes 8 | solution.py:1014
  2.3 93.6 %branch_1_fun.1 = bf16[512,512]{1,0:T(8,128)(2,1)S(1)} custom-call(bf16[128,2048]{1,0:T(8,128)(2,1)} %bitcast.20, bf16[1,2048]{1,0:T(2,128)(2,1)} %get-tuple-element.69.gain, bf16[2048,1280]{1,0:T(8,128)(2,1)} %bitcast.14, bf16[1024,2048]{1,0:T(8,128)(2,1)} %bitcast.16, bf16[2048,256]{1,0:T(8,128)(2,1)} %bitcast.18, s32[4,128]{1,0:T(4,128)} %bitcast.23, ...), custom_call_target="tpu_custom_call" | custom-call | tf_op jit(solution)/shard_map/cond/branch_1_fun/pallas_call | solution.py:959
  95.8 0.8 copy.25
  (1 shorter events, 0.0 us)

commit v4 on v3

--- a/solution.py
+++ b/solution.py
@@ -14,11 +14,13 @@
 CHUNKS = MICRO * PARTS
 CONTEXT = 16
 SORTED = 4
+FIRST = 8
 KEEP = 16
-MAIN = 8
-DEEP = MAIN + 1
-TOTAL = DEEP + MAIN
-POSITION = ((0, 1, 9, 10), (2, 4, 11, 13), (6, 7, 15, 16), (3, 5, 12, 14))
+POSITION = ((0, 1, 10, 11), (3, 7, 13, 16), (4, 8, 14, 17), (2, 6, 12, 15))
+GATHERED = (5, 9)
+DEEPEST = 6
+DEEP = 10
+TOTAL = 18
 LAG_A = 1
 LAG_U = 2
 EPSILON = 1e-05
@@ -388,7 +390,6 @@
     outb,
     hid,
     staged,
-    own_pick,
     late_pick,
     target,
     settled,
@@ -422,7 +423,12 @@
     head = (width - query_width) // 2
     heads = query_width // head
     context = CONTEXT
-    count = DEEP + MAIN * ((last - y) // last)
+    passing = DEEP - (DEEP - DEEPEST) * (y // (last - 1))
+    count = (
+        DEEP
+        + (TOTAL - DEEP) * ((last - y) // last)
+        - (DEEP - DEEPEST) * (y // last)
+    )
     total_width = span * shards * layers
 
     def remote(src, dst, send_sem, recv_sem, target):
@@ -480,85 +486,34 @@
     lane_rank = ((t1 >> 5) << 3) + (t1 & 7)
     slot_row = lax.broadcasted_iota(jnp.int32, (rows, TAIL), 0)
     low_half = t1 < BLOCK
-    base_lane = jnp.zeros((1, TAIL), jnp.int32)
-    base_column = jnp.zeros((TAIL, 1), jnp.int32)
-    late = jnp.zeros((rows, 3 * TAIL), F32)
-
-    def piece_row(ref, p):
-        first = jnp.broadcast_to(ref[p // 2 : p // 2 + 1, :], wide)
-        second = jnp.broadcast_to(ref[p // 2 + 2 : p // 2 + 3, :], wide)
-        if p % 2 == 0:
-            return jnp.where(low_half, first, pltpu.roll(second, BLOCK, 1))
-        return jnp.where(low_half, pltpu.roll(first, BLOCK, 1), second)
-
     def number(mask):
         return jnp.where(mask, 1.0, 0.0)
 
-    for p in range(layers):
-        exit_row = piece_row(exit_rows, p)
-        exit_column = exit_row.T
-        length_column = piece_row(length_rows, p).T
+    def piece_row(ref, p):
+        first = jnp.broadcast_to(ref[pl.ds(p // 2, 1), :], wide)
+        second = jnp.broadcast_to(ref[pl.ds(p // 2 + 2, 1), :], wide)
+        even = jnp.where(low_half, first, pltpu.roll(second, BLOCK, 1))
+        odd = jnp.where(low_half, pltpu.roll(first, BLOCK, 1), second)
+        if isinstance(p, int):
+            return odd if p % 2 else even
+        parity = p % 2
+        return even * (1 - parity) + odd * parity
+
+    def rank_of(exit_row, exit_column):
         ahead = same & (
             (exit_column > exit_row) | ((exit_column == exit_row) & (t0 < t1))
         )
         rank_lane = jnp.sum(number(ahead), axis=0, keepdims=True).astype(jnp.int32)
-        behind = same & (
-            (exit_row > exit_column) | ((exit_row == exit_column) & (t1 < t0))
-        )
-        rank_column = jnp.sum(number(behind), axis=1, keepdims=True).astype(jnp.int32)
-        deep_column = jnp.sum(
-            number(same & (exit_row > 1)), axis=1, keepdims=True
-        ).astype(jnp.int32)
-        deep_lane = jnp.sum(
-            number((exit_column > 1) & (g0 == lane_group)), axis=0, keepdims=True
-        ).astype(jnp.int32)
         order_lane = ((rank_lane >> 3) << 5) + (g1 << 3) + (rank_lane & 7)
-        order_column = ((rank_column >> 3) << 5) + (g0 << 3) + (rank_column & 7)
-        pick = number(order_lane == t0).astype(BF16)
-
-        @pl.when(y == (layers - p) % layers)
-        def _():
-            own_pick[...] = pick
-
-        natural = ((p + layers * (t0 >> 6)) << 4) + (t0 & 15)
-        facts = jnp.concatenate([exit_column, length_column, natural], axis=1)
-        sorted_facts = jnp.dot(
-            pick, facts.astype(F32).astype(BF16), preferred_element_type=F32
-        )
-        for c in range(SORTED):
-            block = sorted_facts[c * rows : (c + 1) * rows].astype(jnp.int32)
-            block = block.reshape(shards, group, 3 * TAIL)
-            exits[POSITION[p][c]] = block[:, :, :TAIL]
-            lens[POSITION[p][c]] = block[:, :, TAIL : 2 * TAIL]
-            starts[POSITION[p][c]] = block[:, :, 2 * TAIL :] * context
-        chosen = (
-            (lane_rank[:rows] >= KEEP)
-            & (lane_rank[:rows] < deep_lane)
-            & (lane_group[:rows] == (slot_row >> 3))
-            & (base_lane + lane_rank[:rows] - KEEP == (slot_row & 7))
-        )
-        chosen = number(chosen).astype(BF16)
-        late_pick[p] = chosen
-        late = late + jnp.dot(
-            chosen, sorted_facts.astype(BF16), preferred_element_type=F32
-        )
-        moved = (rank_column >= KEEP) & (rank_column < deep_column)
-        target[p] = jnp.where(
-            moved,
-            TAIL + (g0 << 3) + base_column + rank_column - KEEP,
-            order_column,
-        )
-        base_lane = base_lane + jnp.maximum(deep_lane - KEEP, 0)
-        base_column = base_column + jnp.maximum(deep_column - KEEP, 0)
-    late = late.astype(jnp.int32).reshape(shards, group, 3 * TAIL)
-    exits[MAIN] = late[:, :, :TAIL]
-    lens[MAIN] = late[:, :, TAIL : 2 * TAIL]
-    starts[MAIN] = late[:, :, 2 * TAIL :] * context
+        return number(order_lane == t0).astype(BF16)
+
+    own_row = piece_row(exit_rows, (layers - y) % layers)
+    own_pick = rank_of(own_row, own_row.T)
 
     hid_copy.wait()
     for j in range(layers):
         ordered = jnp.dot(
-            own_pick[...],
+            own_pick,
             hid[:, j * span : (j + 1) * span],
             preferred_element_type=F32,
         )
@@ -582,31 +537,112 @@
             staged.at[c, j], inb.at[i, j], hid_ss.at[c, j], in_rs.at[i, j], x
         )
 
-    def hidden_start(p, chunks):
-        for c in chunks:
-            for j in range(layers):
-                hidden_copy(p, c, j).start()
-
-    def hidden_sent(p, chunks):
-        for c in chunks:
-            for j in range(layers):
-                hidden_copy(p, c, j).wait_send()
-
-    for p in (1, 3):
-
-        @pl.when(y == layers - p)
-        def _():
-            hidden_start(p, (0, 1))
-            hidden_sent(p, (0, 1))
-            pl.semaphore_signal(
-                turn, inc=1, device_id={"section": 2 * shards + x}, device_id_type=MESH
-            )
-            hidden_start(p, (2, 3))
+    def hidden_start(p, c):
+        for j in range(layers):
+            hidden_copy(p, c, j).start()
+
+    def hidden_sent(p, c, pieces):
+        for j in pieces:
+            hidden_copy(p, c, j).wait_send()
+
+    every = range(layers)
+
+    def next_turn():
+        pl.semaphore_signal(
+            turn, inc=1, device_id={"section": me - shards}, device_id_type=MESH
+        )
+
+    @pl.when(y == 1)
+    def _():
+        for c in range(2):
+            hidden_start(3, c)
+            hidden_sent(3, c, every)
+        for c in range(2, SORTED):
+            hidden_start(3, c)
 
     @pl.when(y == 2)
     def _():
-        pl.semaphore_wait(turn, 2)
-        hidden_start(2, (0, 1, 2, 3))
+        for c in range(2):
+            pl.semaphore_wait(turn, 1)
+            hidden_start(2, c)
+        pl.semaphore_wait(turn, 1)
+        for c in range(2, SORTED):
+            hidden_start(2, c)
+
+    @pl.when(y == 3)
+    def _():
+        hidden_start(1, 0)
+        hidden_sent(1, 0, every[:2])
+        next_turn()
+        hidden_sent(1, 0, every[2:])
+        hidden_start(1, 1)
+        hidden_sent(1, 1, every[:1])
+        next_turn()
+        hidden_sent(1, 1, every[1:])
+        next_turn()
+        for c in range(2, SORTED):
+            hidden_start(1, c)
+
+    def prepare():
+        kinds = ((FIRST, last), (KEEP, 1))
+        base_lane = [jnp.zeros((1, TAIL), jnp.int32) for _ in kinds]
+        base_column = [jnp.zeros((TAIL, 1), jnp.int32) for _ in kinds]
+        late = [jnp.zeros((rows, 3 * TAIL), F32) for _ in kinds]
+
+        for p in range(layers):
+            exit_row = piece_row(exit_rows, p)
+            exit_column = exit_row.T
+            length_column = piece_row(length_rows, p).T
+            pick = rank_of(exit_row, exit_column)
+            behind = same & (
+                (exit_row > exit_column) | ((exit_row == exit_column) & (t1 < t0))
+            )
+            rank_column = jnp.sum(number(behind), axis=1, keepdims=True).astype(jnp.int32)
+            order_column = ((rank_column >> 3) << 5) + (g0 << 3) + (rank_column & 7)
+            natural = ((p + layers * (t0 >> 6)) << 4) + (t0 & 15)
+            facts = jnp.concatenate([exit_column, length_column, natural], axis=1)
+            sorted_facts = jnp.dot(
+                pick, facts.astype(F32).astype(BF16), preferred_element_type=F32
+            )
+            for c in range(SORTED):
+                block = sorted_facts[c * rows : (c + 1) * rows].astype(jnp.int32)
+                block = block.reshape(shards, group, 3 * TAIL)
+                exits[POSITION[p][c]] = block[:, :, :TAIL]
+                lens[POSITION[p][c]] = block[:, :, TAIL : 2 * TAIL]
+                starts[POSITION[p][c]] = block[:, :, 2 * TAIL :] * context
+            goal = order_column
+            for n, (first, depth) in reversed(list(enumerate(kinds))):
+                deep_column = jnp.sum(
+                    number(same & (exit_row > depth)), axis=1, keepdims=True
+                ).astype(jnp.int32)
+                deep_lane = jnp.sum(
+                    number((exit_column > depth) & (g0 == lane_group)), axis=0, keepdims=True
+                ).astype(jnp.int32)
+                ranked = lane_rank[:rows]
+                chosen = (
+                    (ranked >= first)
+                    & (ranked < deep_lane)
+                    & (lane_group[:rows] == (slot_row >> 3))
+                    & (base_lane[n] + ranked - first == (slot_row & 7))
+                )
+                chosen = number(chosen).astype(BF16)
+                late_pick[n, p] = chosen
+                late[n] = late[n] + jnp.dot(
+                    chosen, sorted_facts.astype(BF16), preferred_element_type=F32
+                )
+                goal = jnp.where(
+                    (rank_column >= first) & (rank_column < deep_column),
+                    TAIL + n * rows + (g0 << 3) + base_column[n] + rank_column - first,
+                    goal,
+                )
+                base_lane[n] = base_lane[n] + jnp.maximum(deep_lane - first, 0)
+                base_column[n] = base_column[n] + jnp.maximum(deep_column - first, 0)
+            target[p] = goal
+        for n, i in enumerate(GATHERED):
+            block = late[n].astype(jnp.int32).reshape(shards, group, 3 * TAIL)
+            exits[i] = block[:, :, :TAIL]
+            lens[i] = block[:, :, TAIL : 2 * TAIL]
+            starts[i] = block[:, :, 2 * TAIL :] * context
 
     def rs_copy(i, d):
         target = (x + d) % shards
@@ -657,22 +693,24 @@
             outb.at[i, j], settled.at[i], st_ss.at[i, j], out_rs.at[i], j * shards + x
         )
 
-    def gather_late():
-        for c in range(2, SORTED):
+    def gather_late(n, chunks):
+        for c in chunks:
             for p in range(1, layers):
                 for j in range(layers):
                     state_copy(POSITION[p][c], j).wait_recv()
         for j in range(layers):
             found = None
             for p in range(layers):
-                held = [inb[POSITION[p][c], j].astype(F32) for c in range(2, SORTED)]
-                held = [jnp.zeros_like(part) for part in held] + held
-                held = jnp.concatenate([part.reshape(rows, span) for part in held], axis=0)
-                part = jnp.dot(
-                    late_pick[p], held.astype(BF16), preferred_element_type=F32
-                )
+                held = [
+                    inb[POSITION[p][c], j].astype(F32).reshape(rows, span)
+                    if c in chunks
+                    else jnp.zeros((rows, span), F32)
+                    for c in range(SORTED)
+                ]
+                held = jnp.concatenate(held, axis=0).astype(BF16)
+                part = jnp.dot(late_pick[n, p], held, preferred_element_type=F32)
                 found = part if found is None else found + part
-            inb[MAIN, j] = found.reshape(shards, group, span).astype(BF16)
+            inb[GATHERED[n], j] = found.reshape(shards, group, span).astype(BF16)
 
     def project(i):
         squares = jnp.zeros((rows, TAIL), F32)
@@ -683,7 +721,7 @@
             def _():
                 wq_copies[j].wait()
 
-            @pl.when((y > 0) | ((i > 1) & (i < MAIN)))
+            @pl.when((y > 0) | ((i > 1) & (i < GATHERED[0])))
             def _():
                 state_copy(i, j).wait_recv()
 
@@ -712,15 +750,15 @@
         def _():
             cache_copy.wait()
 
-        b = i - DEEP * (i // DEEP)
-        p = ((b + 6) // 8) * (1 - b // 6) * (1 + 2 * (b % 2)) + 2 * (b // 6)
+        turn = (1 - i // DEEP) * ((i + 2) % layers) + (i // DEEP) * (i % last)
+        p = ((i % DEEP + 8) // DEEP) * ((last - 2 * turn + last * (turn // 2)) % layers)
         half = shards * shards * context
 
-        @pl.when(i == MAIN)
+        @pl.when((i == GATHERED[0]) | (i == GATHERED[1]))
         def _():
             attend_over(i, [(0, cache.shape[0])])
 
-        @pl.when(i != MAIN)
+        @pl.when((i != GATHERED[0]) & (i != GATHERED[1]))
         def _():
             attend_over(
                 i,
@@ -792,7 +830,7 @@
             ag_arrival(i, d).wait_recv()
         attended = att[i].astype(F32).reshape(rows, query_width).astype(BF16)
         depth = exits[i].reshape(rows, TAIL)
-        final = ((y == last) & (i < DEEP)) | (i >= DEEP)
+        final = (y == last) | (i >= passing)
         active = jnp.concatenate([depth] * (span // TAIL), axis=1) > y
         for j in range(layers):
 
@@ -806,7 +844,7 @@
             updated = updated.reshape(shards, group, span).astype(BF16)
             outb[i, j] = updated
 
-            @pl.when((y < last) & (i < DEEP))
+            @pl.when((y < last) & (i < passing))
             def _():
                 state_copy(i, j).start()
 
@@ -819,14 +857,22 @@
                 settled[i] = updated
 
     def step(i, carry):
-        @pl.when((y == 0) & (i == MAIN))
-        def _():
-            gather_late()
+        @pl.when((y == 0) & (i == GATHERED[0]))
+        def _():
+            gather_late(0, (1,))
+
+        @pl.when((y == 0) & (i == GATHERED[1]))
+        def _():
+            gather_late(1, (2, 3))
 
         @pl.when(i < count)
         def _():
             project(i)
 
+        @pl.when(i == LAG_A)
+        def _():
+            prepare()
+
         @pl.when((i >= LAG_A) & (i < count + LAG_A))
         def _():
             attend(i - LAG_A)
@@ -840,7 +886,11 @@
     lax.fori_loop(0, count + LAG_U, step, 0)
 
     def arrive(i, carry):
-        @pl.when(((y != last) & (i < DEEP)) | ((y != 0) & (i >= DEEP)))
+        @pl.when(
+            ((y != last) & (i < DEEPEST))
+            | ((y != last - 1) & (i >= DEEPEST) & (i < DEEP))
+            | ((y != 0) & (i >= DEEP))
+        )
         def _():
             result_copy(i, 0).wait_recv()
 
@@ -849,8 +899,8 @@
     lax.fori_loop(0, TOTAL, arrive, 0)
 
     reach = lax.broadcasted_iota(jnp.int32, wide, 1)
-    extra = settled[MAIN].astype(F32).reshape(rows, span)
-    extra = jnp.concatenate([extra] + [jnp.zeros_like(extra)] * (SORTED - 1), axis=0)
+    extra = [settled[i].astype(F32).reshape(rows, span) for i in GATHERED]
+    extra = jnp.concatenate(extra + [jnp.zeros((2 * rows, span), F32)], axis=0)
     extra = extra.astype(BF16)
     for p in range(layers):
         found = jnp.concatenate(
@@ -874,10 +924,10 @@
         for d in range(1, shards):
             rs_copy(i, d).wait_send()
             ag_copy(i, d).wait_send()
-        final = ((y == last) & (i < DEEP)) | (i >= DEEP)
+        final = (y == last) | (i >= passing)
         for j in range(layers):
 
-            @pl.when((y < last) & (i < DEEP))
+            @pl.when((y < last) & (i < passing))
             def _():
                 state_copy(i, j).wait_send()
 
@@ -889,15 +939,17 @@
 
     lax.fori_loop(0, count, finish, 0)
 
-    for p in (1, 3):
+    for p in range(1, layers):
 
         @pl.when(y == layers - p)
         def _():
-            hidden_sent(p, (2, 3))
+            for c in range(2, SORTED):
+                hidden_sent(p, c, every)
 
     @pl.when(y == 2)
     def _():
-        hidden_sent(2, (0, 1, 2, 3))
+        for c in range(2):
+            hidden_sent(2, c, every)
 
 
 def full(shards, layers, hidden, gain, proj_weight, out_weight, cache, exits, lens):
@@ -969,8 +1021,7 @@
             pltpu.VMEM((TOTAL, layers, shards, group, span), BF16),
             pltpu.VMEM(hidden.shape, BF16),
             pltpu.VMEM((SORTED, layers, shards, group, span), BF16),
-            pltpu.VMEM((TAIL, TAIL), BF16),
-            pltpu.VMEM((layers, rows, TAIL), BF16),
+            pltpu.VMEM((2, layers, rows, TAIL), BF16),
             pltpu.VMEM((layers, TAIL, TAIL), jnp.int32),
             pltpu.VMEM((TOTAL, shards, group, span), BF16),
             pltpu.VMEM(fact, jnp.int32),
@@ -1007,10 +1058,14 @@
     exits = exit_layer.reshape(tokens // TAIL, TAIL)
     lens = lengths.reshape(tokens // TAIL, TAIL)
     operands = (hidden[0], norm_gain, w_qkv[0], w_out[0], cache, exits, lens)
-    going = (exit_layer > 1).astype(jnp.int32)
-    going = going.reshape(MICRO // layers, layers, shards, BLOCK // shards)
-    over = jnp.maximum(jnp.sum(going, axis=(0, 3)) - KEEP, 0)
-    fits = jnp.max(jnp.sum(over, axis=0)) <= BLOCK // shards // PARTS
+    held = exit_layer.reshape(MICRO // layers, layers, shards, BLOCK // shards)
+
+    def beyond(depth, first):
+        deep = jnp.sum((held > depth).astype(jnp.int32), axis=(0, 3))
+        return jnp.sum(jnp.maximum(deep - first, 0), axis=0)
+
+    over = jnp.maximum(beyond(layers - 1, FIRST), beyond(1, KEEP))
+    fits = jnp.max(over) <= BLOCK // shards // PARTS
     return lax.cond(
         fits,
         functools.partial(early, shards, layers),

time: 97 us -> 87.3 us (0.900)
  Pallas kernels: 93.6 us -> 83.9 us
    pallas_call x1, Pallas kernels: 93.6 us -> 83.9 us  [early(): pl.pallas_call(functools.partial(early_kernel, shards, layers), out_shape...]
where the time goes in v4:
time: 87.3 us; the launch traced here: 87.2 us
  Pallas kernels  83.9 us (96%)
  other arithmetic  1.66 us (2%)
  local copies, waits for them, and re-layouts  0.97 us (1%)
    pallas_call x1, Pallas kernels, early(): pl.pallas_call(functools.partial(early_kernel, shards, layers), out_shape...  83.9 us

profile of v4, /device:TPU:32, one launch (start us, length us, event | category | flops | bytes accessed | tf_op | source)
XLA Modules:
  0.0 87.2 jit_solution(12948200515403073807)
XLA Ops:
  0.0 0.7 compare_convert_fusion
  0.7 0.1 reshape.31
  0.8 0.2 reduce_sum.38
  0.9 0.1 reshape.30
  1.0 0.2 reduce_sum.36
  1.2 0.6 maximum_reduce_fusion.2
  2.5 83.9 %conditional.1 = (bf16[512,512]{1,0:T(8,128)(2,1)S(1)}) conditional(s32[]{:T(128)} %convert_element_type.19, (bf16[1,128,2048]{2,1,0:T(8,128)(2,1)}, bf16[1,2048]{1,0:T(2,128)(2,1)}, bf16[1,2048,1280]{2,1,0:T(8,128)(2,1)}, bf16[1,1024,2048]{2,1,0:T(8,128)(2,1)}, bf16[1,128,16,256]{3,2,1,0:T(8,128)(2,1)}, /*index=5*/s32[512]{0:T(512)}, ...), branch_computations={%region_5.0_spmd, %region_6.0_spmd} | conditional | bytes 8 | solution.py:1069
  2.5 83.9 %branch_1_fun.1 = bf16[512,512]{1,0:T(8,128)(2,1)S(1)} custom-call(bf16[128,2048]{1,0:T(8,128)(2,1)} %bitcast.20, bf16[1,2048]{1,0:T(2,128)(2,1)} %get-tuple-element.69.gain, bf16[2048,1280]{1,0:T(8,128)(2,1)} %bitcast.14, bf16[1024,2048]{1,0:T(8,128)(2,1)} %bitcast.16, bf16[2048,256]{1,0:T(8,128)(2,1)} %bitcast.18, s32[4,128]{1,0:T(4,128)} %bitcast.23, ...), custom_call_target="tpu_custom_call" | custom-call | tf_op jit(solution)/shard_map/cond/branch_1_fun/pallas_call | solution.py:1011
  86.4 0.8 copy.25
  (1 shorter events, 0.0 us)

commit v5 on v4

--- a/solution.py
+++ b/solution.py
@@ -18,6 +18,7 @@
 KEEP = 16
 POSITION = ((0, 1, 10, 11), (3, 7, 13, 16), (4, 8, 14, 17), (2, 6, 12, 15))
 GATHERED = (5, 9)
+WAITED = 15
 DEEPEST = 6
 DEEP = 10
 TOTAL = 18
@@ -390,7 +391,9 @@
     outb,
     hid,
     staged,
+    relay,
     late_pick,
+    late_cache,
     target,
     settled,
     exits,
@@ -404,6 +407,8 @@
     hid_in,
     hid_ss,
     turn,
+    relay_ss,
+    relay_rs,
     in_rs,
     rs_ss,
     rs_rs,
@@ -552,21 +557,32 @@
             turn, inc=1, device_id={"section": me - shards}, device_id_type=MESH
         )
 
+    def relay_copy(j):
+        return remote(
+            staged.at[1, j], relay.at[j], hid_ss.at[1, j], relay_rs.at[j], shards + x
+        )
+
+    def relay_on(j):
+        i = POSITION[2][1]
+        return remote(relay.at[j], inb.at[i, j], relay_ss.at[j], in_rs.at[i, j], x)
+
     @pl.when(y == 1)
     def _():
         for c in range(2):
             hidden_start(3, c)
             hidden_sent(3, c, every)
+        for j in every:
+            relay_copy(j).wait_recv()
+            relay_on(j).start()
         for c in range(2, SORTED):
             hidden_start(3, c)
 
     @pl.when(y == 2)
     def _():
-        for c in range(2):
+        for j in every:
+            relay_copy(j).start()
+        for c in (0, 2, 3):
             pl.semaphore_wait(turn, 1)
-            hidden_start(2, c)
-        pl.semaphore_wait(turn, 1)
-        for c in range(2, SORTED):
             hidden_start(2, c)
 
     @pl.when(y == 3)
@@ -575,13 +591,11 @@
         hidden_sent(1, 0, every[:2])
         next_turn()
         hidden_sent(1, 0, every[2:])
-        hidden_start(1, 1)
-        hidden_sent(1, 1, every[:1])
-        next_turn()
-        hidden_sent(1, 1, every[1:])
-        next_turn()
-        for c in range(2, SORTED):
+        for c in (1, 2):
             hidden_start(1, c)
+            hidden_sent(1, c, every)
+            next_turn()
+        hidden_start(1, 3)
 
     def prepare():
         kinds = ((FIRST, last), (KEEP, 1))
@@ -643,6 +657,20 @@
             exits[i] = block[:, :, :TAIL]
             lens[i] = block[:, :, TAIL : 2 * TAIL]
             starts[i] = block[:, :, 2 * TAIL :] * context
+        cache_copy.wait()
+        for n, i in enumerate(GATHERED):
+            source = jnp.broadcast_to(
+                starts[i, x].reshape(group, 1, TAIL), (group, context, TAIL)
+            ).reshape(group * context, TAIL)
+            source = source + lax.broadcasted_iota(jnp.int32, source.shape, 0) % context
+            lane = lax.broadcasted_iota(jnp.int32, source.shape, 1)
+            pick = [
+                number(source == lane + m * TAIL).astype(BF16)
+                for m in range(cache.shape[0] // TAIL)
+            ]
+            late_cache[n] = jnp.dot(
+                jnp.concatenate(pick, axis=1), cache[...], preferred_element_type=F32
+            ).astype(BF16)
 
     def rs_copy(i, d):
         target = (x + d) % shards
@@ -721,7 +749,7 @@
             def _():
                 wq_copies[j].wait()
 
-            @pl.when((y > 0) | ((i > 1) & (i < GATHERED[0])))
+            @pl.when((y > 0) | ((i > 1) & (i < GATHERED[0])) | (i >= WAITED))
             def _():
                 state_copy(i, j).wait_recv()
 
@@ -746,29 +774,38 @@
             rs_copy(i, d).start()
 
     def attend(i):
-        @pl.when(i == 0)
-        def _():
-            cache_copy.wait()
-
         turn = (1 - i // DEEP) * ((i + 2) % layers) + (i // DEEP) * (i % last)
         p = ((i % DEEP + 8) // DEEP) * ((last - 2 * turn + last * (turn // 2)) % layers)
         half = shards * shards * context
+        lane = lax.broadcasted_iota(jnp.int32, (heads * group, TAIL), 1)
 
         @pl.when((i == GATHERED[0]) | (i == GATHERED[1]))
         def _():
-            attend_over(i, [(0, cache.shape[0])])
-
-        @pl.when((i != GATHERED[0]) & (i != GATHERED[1]))
-        def _():
+            n = i // GATHERED[1]
+            row = lax.broadcasted_iota(jnp.int32, (heads * group, TAIL), 0)
             attend_over(
                 i,
+                late_cache[n, :, :head],
+                late_cache[n, :, head:],
+                [lane - (row % group) * context],
+            )
+
+        @pl.when((i != GATHERED[0]) & (i != GATHERED[1]))
+        def _():
+            pieces = [pl.multiple_of(m * half, half) for m in (p, p + layers)]
+            start = jnp.concatenate([starts[i, x]] * heads, axis=0)
+            attend_over(
+                i,
+                jnp.concatenate([cache[pl.ds(at, half), :head] for at in pieces], axis=0),
+                jnp.concatenate([cache[pl.ds(at, half), head:] for at in pieces], axis=0),
                 [
-                    (pl.multiple_of(p * half, half), half),
-                    (pl.multiple_of((p + layers) * half, half), half),
+                    lane + (at + m * TAIL) - start
+                    for at in pieces
+                    for m in range(half // TAIL)
                 ],
             )
 
-    def attend_over(i, pieces):
+    def attend_over(i, keys, values, offset):
 
         summed = accs[i, x]
         for d in (1, 3, 2):
@@ -786,26 +823,11 @@
         value_new = fitted[:, query_width + head :].astype(BF16).astype(F32)
         key_new = jnp.concatenate([key_new] * heads, axis=0)
         value_new = jnp.concatenate([value_new] * heads, axis=0)
-        keys = jnp.concatenate(
-            [cache[pl.ds(at, size), :head] for at, size in pieces], axis=0
-        )
-        values = jnp.concatenate(
-            [cache[pl.ds(at, size), head:] for at, size in pieces], axis=0
-        )
         scores = lax.dot_general(
             query, keys, (((1,), (1,)), ((), ())), preferred_element_type=F32
         )
         own = jnp.sum(query.astype(F32) * key_new, axis=1, keepdims=True)
-        def per_query(fact):
-            return jnp.concatenate([fact[i, x]] * heads, axis=0)
-
-        reach = per_query(lens)
-        start = per_query(starts)
-        offset = []
-        for at, size in pieces:
-            for n in range(size // TAIL):
-                lane = lax.broadcasted_iota(jnp.int32, start.shape, 1)
-                offset.append(lane + (at + n * TAIL) - start)
+        reach = jnp.concatenate([lens[i, x]] * heads, axis=0)
         reach = jnp.concatenate([reach] * len(offset), axis=1)
         offset = jnp.concatenate(offset, axis=1)
         usable = (offset >= 0) & (offset < reach)
@@ -863,7 +885,7 @@
 
         @pl.when((y == 0) & (i == GATHERED[1]))
         def _():
-            gather_late(1, (2, 3))
+            gather_late(1, (2,))
 
         @pl.when(i < count)
         def _():
@@ -873,17 +895,29 @@
         def _():
             prepare()
 
-        @pl.when((i >= LAG_A) & (i < count + LAG_A))
-        def _():
-            attend(i - LAG_A)
-
-        @pl.when(i >= LAG_U)
-        def _():
-            update(i - LAG_U)
+        behind = i - LAG_A - LAG_A * (i // (DEEP + LAG_A))
+
+        @pl.when(
+            (i >= LAG_A)
+            & ((i < DEEP + LAG_A) | (i >= DEEP + 2 * LAG_A))
+            & (behind < count)
+        )
+        def _():
+            attend(behind)
+
+        far_behind = i - LAG_U - LAG_U * (i // (DEEP + LAG_U))
+
+        @pl.when(
+            (i >= LAG_U)
+            & ((i < DEEP + LAG_U) | (i >= DEEP + 2 * LAG_U))
+            & (far_behind < count)
+        )
+        def _():
+            update(far_behind)
 
         return carry
 
-    lax.fori_loop(0, count + LAG_U, step, 0)
+    lax.fori_loop(0, count + LAG_U + LAG_U * ((last - y) // last), step, 0)
 
     def arrive(i, carry):
         @pl.when(
@@ -939,17 +973,23 @@
 
     lax.fori_loop(0, count, finish, 0)
 
-    for p in range(1, layers):
-
-        @pl.when(y == layers - p)
-        def _():
-            for c in range(2, SORTED):
-                hidden_sent(p, c, every)
+    @pl.when(y == 1)
+    def _():
+        for c in range(2, SORTED):
+            hidden_sent(3, c, every)
+        for j in every:
+            relay_on(j).wait_send()
 
     @pl.when(y == 2)
     def _():
-        for c in range(2):
+        for j in every:
+            relay_copy(j).wait_send()
+        for c in (0, 2, 3):
             hidden_sent(2, c, every)
+
+    @pl.when(y == 3)
+    def _():
+        hidden_sent(1, 3, every)
 
 
 def full(shards, layers, hidden, gain, proj_weight, out_weight, cache, exits, lens):
@@ -1021,7 +1061,9 @@
             pltpu.VMEM((TOTAL, layers, shards, group, span), BF16),
             pltpu.VMEM(hidden.shape, BF16),
             pltpu.VMEM((SORTED, layers, shards, group, span), BF16),
+            pltpu.VMEM((layers, shards, group, span), BF16),
             pltpu.VMEM((2, layers, rows, TAIL), BF16),
+            pltpu.VMEM((2, group * CONTEXT, cache.shape[1]), BF16),
             pltpu.VMEM((layers, TAIL, TAIL), jnp.int32),
             pltpu.VMEM((TOTAL, shards, group, span), BF16),
             pltpu.VMEM(fact, jnp.int32),
@@ -1035,6 +1077,8 @@
             dma((1,)),
             dma((SORTED, layers)),
             pltpu.SemaphoreType.REGULAR,
+            dma((layers,)),
+            dma((layers,)),
             dma((TOTAL, layers)),
             dma((TOTAL, shards - 1)),
             dma((TOTAL, shards)),

time: 87.3 us -> 87.5 us (level)
  no operation moved by 1% of the time
where the time goes in v5:
time: 87.5 us; the launch traced here: 87.3 us
  Pallas kernels  84 us (96%)
  other arithmetic  1.66 us (2%)
  local copies, waits for them, and re-layouts  0.97 us (1%)
    pallas_call x1, Pallas kernels, early(): pl.pallas_call(functools.partial(early_kernel, shards, layers), out_shape...  84 us

profile of v5, /device:TPU:32, one launch (start us, length us, event | category | flops | bytes accessed | tf_op | source)
XLA Modules:
  0.0 87.3 jit_solution(18271787195081457372)
XLA Ops:
  0.0 0.7 compare_convert_fusion
  0.7 0.1 reshape.31
  0.8 0.2 reduce_sum.38
  0.9 0.1 reshape.30
  1.0 0.2 reduce_sum.36
  1.2 0.6 maximum_reduce_fusion.2
  2.5 84.0 %conditional.1 = (bf16[512,512]{1,0:T(8,128)(2,1)S(1)}) conditional(s32[]{:T(128)} %convert_element_type.19, (bf16[1,128,2048]{2,1,0:T(8,128)(2,1)}, bf16[1,2048]{1,0:T(2,128)(2,1)}, bf16[1,2048,1280]{2,1,0:T(8,128)(2,1)}, bf16[1,1024,2048]{2,1,0:T(8,128)(2,1)}, bf16[1,128,16,256]{3,2,1,0:T(8,128)(2,1)}, /*index=5*/s32[512]{0:T(512)}, ...), branch_computations={%region_5.0_spmd, %region_6.0_spmd} | conditional | bytes 8 | solution.py:1113
  2.5 84.0 %branch_1_fun.1 = bf16[512,512]{1,0:T(8,128)(2,1)S(1)} custom-call(bf16[128,2048]{1,0:T(8,128)(2,1)} %bitcast.20, bf16[1,2048]{1,0:T(2,128)(2,1)} %get-tuple-element.69.gain, bf16[2048,1280]{1,0:T(8,128)(2,1)} %bitcast.14, bf16[1024,2048]{1,0:T(8,128)(2,1)} %bitcast.16, bf16[2048,256]{1,0:T(8,128)(2,1)} %bitcast.18, s32[4,128]{1,0:T(4,128)} %bitcast.23, ...), custom_call_target="tpu_custom_call" | custom-call | tf_op jit(solution)/shard_map/cond/branch_1_fun/pallas_call | solution.py:1051
  86.5 0.8 copy.25
  (1 shorter events, 0.0 us)
